TPU v7x, 32 devices: a 4x4x1 block of a 4x4x8 slice. The times are simulated.
32 devices in a mesh: dp: 1 (over z), tp: 4 (over y), ep: 8 (over x, core).
Axes of the slice: x: 4, y: 4, z: 1, core: 2. Of those that a mesh axis runs over, the one named last changes fastest.
The devices are a block of a 4x4x8 slice.
Arguments:
- x_in: bfloat16 [2048, 1536], P(('dp', 'ep', 'tp'))
- norm_gain: bfloat16 [1536], replicated
- w_router: bfloat16 [1536, 40], replicated
- expert_idx: int32 [2048, 8], P(('dp', 'ep', 'tp'))
- w_gate: bfloat16 [40, 1536, 512], P('ep', None, 'tp')
- w_up: bfloat16 [40, 1536, 512], P('ep', None, 'tp')
- w_down: bfloat16 [40, 512, 1536], P('ep', 'tp')
- out_bias: bfloat16 [1536], replicated
- dy_out: bfloat16 [2048, 1536], P(('dp', 'ep', 'tp'))
Outputs:
- output 1: bfloat16 [2048, 1536], P(('dp', 'ep', 'tp'))
- output 2: bfloat16 [2048, 1536], P(('dp', 'ep', 'tp'))
- output 3: float32 [1536], P('dp')
- output 4: float32 [1536, 40], P('dp')
- output 5: float32 [40, 1536, 512], P(('dp', 'ep'), None, 'tp')
- output 6: float32 [40, 1536, 512], P(('dp', 'ep'), None, 'tp')
- output 7: float32 [40, 512, 1536], P(('dp', 'ep'), 'tp')
- output 8: float32 [1536], P('dp')
All inputs are finite; a program needn't handle non-finite values.
Results may differ from a plain program's by a relative error of at most 0.0116395.
Values are sent between devices in bfloat16 or wider.
A program may use at most 768 MiB of HBM per device.

v0:
```python
import jax
import jax.numpy as jnp
from jax import lax
from jax.sharding import PartitionSpec as P

EPS = 1e-6


def routing_tables(expert_ids, n_exp, capacity):
    n_tok, top_k = expert_ids.shape
    flat_ids = expert_ids.reshape(-1)
    order = jnp.argsort(flat_ids, stable=True)
    counts = jnp.sum((flat_ids[:, None] == jnp.arange(n_exp)[None, :]).astype(jnp.int32), axis=0)
    starts = jnp.cumsum(counts) - counts
    slot_rank = jnp.arange(capacity)[None, :]
    slot_copy = order[jnp.minimum(starts[:, None] + slot_rank, n_tok * top_k - 1)]
    slot_ok = slot_rank < counts[:, None]
    copy_pos = flat_ids * capacity + jnp.argsort(order) - starts[flat_ids]
    return slot_copy, slot_ok, copy_pos.reshape(n_tok, top_k)


def solution(mesh):
    tok_spec = P(("dp", "ep", "tp"), None)
    wide_spec = P("ep", None, "tp")
    down_spec = P("ep", "tp", None)
    grad_wide = P(("dp", "ep"), None, "tp")
    grad_down = P(("dp", "ep"), "tp", None)

    def device_step(x_in, norm_gain, w_router, expert_idx, w_gate, w_up, w_down, out_bias, dy_out):
        n_tok, d_model = x_in.shape
        n_exp = w_router.shape[1]
        top_k = expert_idx.shape[1]
        local_exp = w_gate.shape[0]
        n_ep = n_exp // local_exp
        capacity = (2 * n_tok * top_k + n_exp - 1) // n_exp
        x_f32 = x_in.astype(jnp.float32)
        inv_rms = lax.rsqrt(jnp.mean(x_f32 * x_f32, axis=-1, keepdims=True) + EPS)
        normed = x_f32 * inv_rms
        gain_f32 = norm_gain.astype(jnp.float32)
        hidden = (normed * gain_f32).astype(jnp.bfloat16)
        logits = jnp.dot(hidden, w_router, preferred_element_type=jnp.float32)
        chosen = expert_idx[:, :, None] == jnp.arange(n_exp)[None, None, :]
        gates = jax.nn.softmax(jnp.sum(jnp.where(chosen, logits[:, None, :], 0.0), axis=-1), axis=-1)
        slot_copy, slot_ok, copy_pos = routing_tables(expert_idx, n_exp, capacity)
        place_shape = (n_ep, local_exp, capacity, d_model)
        send_rows = jnp.where(slot_ok[:, :, None], hidden[slot_copy // top_k], 0).reshape(place_shape)
        recv_rows = lax.all_to_all(send_rows, "ep", 0, 0, tiled=True)
        rows_in = lax.all_gather(recv_rows, "tp", axis=0)
        gate_pre = jnp.einsum("tsmcd,mdf->tsmcf", rows_in, w_gate, preferred_element_type=jnp.float32)
        up_pre = jnp.einsum("tsmcd,mdf->tsmcf", rows_in, w_up, preferred_element_type=jnp.float32)
        sigma_gate = jax.nn.sigmoid(gate_pre)
        silu_gate = gate_pre * sigma_gate
        hidden_act = (silu_gate * up_pre).astype(jnp.bfloat16)
        part_out = jnp.einsum("tsmcf,mfd->tsmcd", hidden_act, w_down, preferred_element_type=jnp.float32).astype(jnp.bfloat16)
        y_recv = lax.psum_scatter(part_out, "tp", scatter_dimension=0, tiled=True)[0]
        y_slots = lax.all_to_all(y_recv, "ep", 0, 0, tiled=True).reshape(n_exp * capacity, d_model)
        y_copy = y_slots[copy_pos].astype(jnp.float32)
        moe_out = jnp.sum(gates[:, :, None] * y_copy, axis=1) + out_bias.astype(jnp.float32)
        y_out = (x_f32 + moe_out).astype(jnp.bfloat16)
        dy_f32 = dy_out.astype(jnp.float32)
        d_bias = jnp.sum(dy_f32, axis=0)
        d_gates = jnp.sum(dy_f32[:, None, :] * y_copy, axis=-1)
        dy_copy = (gates[:, :, None] * dy_f32[:, None, :]).astype(jnp.bfloat16).reshape(n_tok * top_k, d_model)
        d_send = jnp.where(slot_ok[:, :, None], dy_copy[slot_copy], 0).reshape(place_shape)
        d_recv = lax.all_to_all(d_send, "ep", 0, 0, tiled=True)
        d_rows = lax.all_gather(d_recv, "tp", axis=0)
        d_act = jnp.einsum("tsmcd,mfd->tsmcf", d_rows, w_down, preferred_element_type=jnp.float32)
        d_down = jnp.einsum("tsmcf,tsmcd->mfd", hidden_act, d_rows, preferred_element_type=jnp.float32)
        d_gate_pre = (d_act * up_pre * sigma_gate * (1.0 + gate_pre * (1.0 - sigma_gate))).astype(jnp.bfloat16)
        d_up_pre = (d_act * silu_gate).astype(jnp.bfloat16)
        d_gate = jnp.einsum("tsmcd,tsmcf->mdf", rows_in, d_gate_pre, preferred_element_type=jnp.float32)
        d_up = jnp.einsum("tsmcd,tsmcf->mdf", rows_in, d_up_pre, preferred_element_type=jnp.float32)
        dh_part = (jnp.einsum("tsmcf,mdf->tsmcd", d_gate_pre, w_gate, preferred_element_type=jnp.float32) + jnp.einsum("tsmcf,mdf->tsmcd", d_up_pre, w_up, preferred_element_type=jnp.float32)).astype(jnp.bfloat16)
        dh_recv = lax.psum_scatter(dh_part, "tp", scatter_dimension=0, tiled=True)[0]
        dh_slots = lax.all_to_all(dh_recv, "ep", 0, 0, tiled=True).reshape(n_exp * capacity, d_model)
        dh_expert = jnp.sum(dh_slots[copy_pos].astype(jnp.float32), axis=1)
        d_chosen = gates * (d_gates - jnp.sum(gates * d_gates, axis=-1, keepdims=True))
        d_logits = jnp.sum(jnp.where(chosen, d_chosen[:, :, None], 0.0), axis=1)
        d_router = jnp.einsum("td,te->de", hidden, d_logits, preferred_element_type=jnp.float32)
        dh_total = dh_expert + jnp.einsum("te,de->td", d_logits, w_router, preferred_element_type=jnp.float32)
        d_gain = jnp.sum(dh_total * normed, axis=0)
        d_norm = dh_total * gain_f32
        dx_in = (dy_f32 + inv_rms * (d_norm - normed * jnp.mean(d_norm * normed, axis=-1, keepdims=True))).astype(jnp.bfloat16)
        d_gain, d_router, d_bias = lax.psum((d_gain, d_router, d_bias), ("ep", "tp"))
        return y_out, dx_in, d_gain, d_router, d_gate, d_up, d_down, d_bias

    return jax.shard_map(device_step, mesh=mesh, in_specs=(tok_spec, P(None), P(None, None), tok_spec, wide_spec, wide_spec, down_spec, P(None), tok_spec), out_specs=(tok_spec, tok_spec, P("dp"), P("dp", None), grad_wide, grad_wide, grad_down, P("dp")), check_vma=False)
```

profile of v0, /device:TPU:97, one launch (start us, length us, event | category | flops | bytes accessed | tf_op | source)
XLA Modules:
  0.0 779.2 jit_solution(2319597814361160232)
XLA Ops:
  7.3 1.2 fusion.52
  8.5 0.7 convert_element_type.59
  9.2 0.8 copy.83
  10.2 3.8 sort.34
  14.5 0.1 reshape.364
  14.7 6.9 gather_fusion
  22.2 0.2 fusion.61
  22.5 0.5 copy-done.21
  23.2 0.7 copy-done.8
  24.0 1.4 fusion.18
  25.3 10.2 %gather_fusion.3 = bf16[1040,1536]{1,0:T(8,128)(2,1)} fusion(bf16[512,1536]{1,0:T(8,128)(2,1)} %fusion.18, s32[2048]{0:T(1024)S(1)} %pad_clamp_fusion), kind=kCustom, calls=%fused_computation.3 | custom fusion | bytes 6393920 | tf_op jit(solution)/shard_map/gather | solution.py:64
  35.6 5.5 gather.31
  41.1 5.2 gather_fusion.1
  46.2 5.5 gather.27
  51.7 4.9 broadcast_select_fusion
  56.6 51.6 %all_to_all.20 = bf16[8,5,26,1536]{3,2,1,0:T(8,128)(2,1)S(1)} all-to-all(bf16[8,5,26,1536]{3,2,1,0:T(8,128)(2,1)S(1)} %get-tuple-element.62), channel_id=1, replica_groups=mesh['dp'=1,'tp'=4,'ep'=8] {'ep'}, dimensions={0} | all-to-all | bytes 6389760 | tf_op jit(solution)/shard_map/all_to_all | solution.py:47
  108.2 3.5 copy.85
  111.8 50.4 %all_to_all.21 = bf16[8,5,26,1536]{3,2,1,0:T(8,128)(2,1)S(1)} all-to-all(bf16[8,5,26,1536]{3,2,1,0:T(8,128)(2,1)} %get-tuple-element.61), channel_id=1, replica_groups=mesh['dp'=1,'tp'=4,'ep'=8] {'ep'}, dimensions={0} | all-to-all | bytes 6389760 | tf_op jit(solution)/shard_map/all_to_all | solution.py:65
  162.3 3.5 copy.91
  165.8 0.3 reduce-scatter.3.cloned.1.call-start
  166.1 65.3 %all-gather.5.cloned.1.call-done = bf16[32,5,26,1536]{3,0,2,1:T(8,128)(2,1)} async-done(((bf16[8,5,26,1536]{3,0,2,1:T(8,128)(2,1)}), bf16[32,5,26,1536]{3,0,2,1:T(8,128)(2,1)}) %all-gather.5.cloned.1.call-update) | async-done | bytes 12779536 | tf_op jit(solution)/shard_map/all_gather | solution.py:48
  231.4 14.7 %copy.86 = bf16[32,5,26,1536]{3,2,0,1:T(8,128)(2,1)} copy(bf16[32,5,26,1536]{3,0,2,1:T(8,128)(2,1)} %all-gather.5.cloned.1.call-done) | data formatting | bytes 25559040 | tf_op jit(solution)/shard_map/all_gather | solution.py:48
  246.1 9.3 %fusion.29 = f32[5,4,8,26,128]{4,3,2,1,0:T(8,128)} fusion(bf16[4,8,5,26,1536]{4,3,1,0,2:T(8,128)(2,1)} %bitcast.157, bf16[5,1536,128]{2,1,0:T(8,128)(2,1)S(1)} %copy-done.6), kind=kOutput, calls=%fused_computation.43 | convolution fusion | flops 1635778560 | bytes 16875520 | tf_op jit(solution)/shard_map/tsmcd,mdf->tsmcf/dot_general | solution.py:50
  255.4 9.2 %fusion.33 = f32[5,4,8,26,128]{4,3,2,1,0:T(8,128)} fusion(bf16[4,8,5,26,1536]{4,3,1,0,2:T(8,128)(2,1)} %bitcast.158, bf16[5,1536,128]{2,1,0:T(8,128)(2,1)S(1)} %copy-done.4), kind=kOutput, calls=%fused_computation.47 | convolution fusion | flops 1635778560 | bytes 16875520 | tf_op jit(solution)/shard_map/tsmcd,mdf->tsmcf/dot_general | solution.py:49
  264.6 88.1 %all-gather.7.cloned.1.call-done = bf16[32,5,26,1536]{3,0,2,1:T(8,128)(2,1)} async-done(((bf16[8,5,26,1536]{3,0,2,1:T(8,128)(2,1)}), bf16[32,5,26,1536]{3,0,2,1:T(8,128)(2,1)}) %all-gather.7.cloned.1.call-update) | async-done | bytes 12779536 | tf_op jit(solution)/shard_map/all_gather | solution.py:66
  352.8 14.6 %copy.92 = bf16[32,5,26,1536]{3,2,0,1:T(8,128)(2,1)} copy(bf16[32,5,26,1536]{3,0,2,1:T(8,128)(2,1)} %all-gather.7.cloned.1.call-done) | data formatting | bytes 25559040 | tf_op jit(solution)/shard_map/all_gather | solution.py:66
  367.3 13.2 %fusion.22 = (bf16[4,8,5,26,128]{4,3,1,0,2:T(8,128)(2,1)}, bf16[4,8,5,26,128]{4,3,1,0,2:T(8,128)(2,1)}, bf16[4,8,5,26,128]{4,3,1,0,2:T(8,128)(2,1)S(1)}) fusion(f32[5,4,8,26,128]{4,3,2,1,0:T(8,128)} %fusion.33, f32[5,4,8,26,128]{4,3,2,1,0:T(8,128)} %fusion.29, bf16[4,8,5,26,1536]{4,3,1,0,2:T(8,128)(2,1)} %bitcast.159, bf16[5,128,1536]{2,1,0:T(8,128)(2,1)S(1)} %copy-done), kind=kOutput, calls=%fused_computation.31 | convolution fusion | flops 1643765760 | bytes 22200320 | tf_op jit(solution)/shard_map/tsmcd,mfd->tsmcf/dot_general | solution.py:67
  380.6 7.7 convert_bitcast_fusion
  388.3 15.7 %copy.87 = bf16[4,8,5,26,1536]{4,1,3,2,0:T(8,128)(2,1)} copy(bf16[4,8,5,26,1536]{4,3,1,0,2:T(8,128)(2,1)} %convert_bitcast_fusion) | data formatting | bytes 25559040 | tf_op jit(solution)/shard_map/convert_element_type | solution.py:54
  404.1 1.4 copy-done.5
  405.5 14.0 %fusion.31 = f32[5,4,8,26,1536]{4,3,2,1,0:T(8,128)} fusion(bf16[4,8,5,26,128]{4,3,1,0,2:T(8,128)(2,1)} %get-tuple-element.54, bf16[5,1536,128]{2,1,0:T(8,128)(2,1)S(1)} %copy-done.5), kind=kOutput, calls=%fused_computation.45 | convolution fusion | flops 1635778560 | bytes 28590080 | tf_op jit(solution)/shard_map/tsmcf,mdf->tsmcd/dot_general | solution.py:73
  419.5 18.0 %fusion.6 = bf16[4,8,5,26,1536]{4,3,1,0,2:T(8,128)(2,1)} fusion(f32[5,4,8,26,1536]{4,3,2,1,0:T(8,128)} %fusion.31, bf16[4,8,5,26,128]{4,3,1,0,2:T(8,128)(2,1)S(1)} %copy-done.14, bf16[5,1536,128]{2,1,0:T(8,128)(2,1)S(1)} %copy-done.7), kind=kOutput, calls=%fused_computation.13 | convolution fusion | flops 1648558080 | bytes 41369600 | tf_op jit(solution)/shard_map/tsmcf,mdf->tsmcd/dot_general | solution.py:73
  437.5 15.3 %copy.93 = bf16[4,8,5,26,1536]{4,1,3,2,0:T(8,128)(2,1)} copy(bf16[4,8,5,26,1536]{4,3,1,0,2:T(8,128)(2,1)} %fusion.6) | data formatting | bytes 25559040 | tf_op jit(solution)/shard_map/convert_element_type | solution.py:73
  452.9 0.5 copy-done.34
  453.4 0.6 convert_element_type.66
  454.0 3.8 sort.35
  457.8 0.6 fusion.60
  458.4 0.7 fusion.58
  459.1 0.7 fusion.59
  459.9 4.4 compare_select_fusion.4
  464.3 0.2 compare_reduce_fusion.32
  464.5 20.7 %select_subtract_fusion = s32[512]{0:T(512)S(1)} fusion(pred[512]{0:T(512)(128)(4,1)S(1)} %get-tuple-element.48, pred[512]{0:T(512)(128)(4,1)S(1)} %get-tuple-element.47, pred[512]{0:T(512)(128)(4,1)S(1)} %get-tuple-element.46, pred[512]{0:T(512)(128)(4,1)S(1)} %get-tuple-element.45, pred[512]{0:T(512)(128)(4,1)S(1)} %get-tuple-element.44, ...), kind=kLoop, calls=%fused_computation.138 | loop fusion | flops 18432 | bytes 25220 | tf_op jit(solution)/shard_map/sub | solution.py:18
  485.4 33.4 %reduce-scatter.3.cloned.1.call-done = bf16[1,8,5,26,1536]{4,1,3,2,0:T(8,128)(2,1)} async-done(((bf16[4,8,5,26,1536]{4,1,3,2,0:T(8,128)(2,1)}), bf16[1,8,5,26,1536]{4,1,3,2,0:T(8,128)(2,1)}) %reduce-scatter.3.cloned.1.call-update) | async-done | bytes 3194896 | tf_op jit(solution)/shard_map/reduce_scatter | solution.py:55
  518.8 4.9 copy.88
  523.7 5.6 all-to-all-start.1
  529.4 14.7 %fusion.13 = f32[5,128,1536]{2,1,0:T(8,128)} fusion(bf16[4,8,5,26,1536]{4,1,0,3,2:T(8,128)(2,1)} %bitcast.164, bf16[4,8,5,26,128]{4,3,1,0,2:T(8,128)(2,1)S(1)} %get-tuple-element.55), kind=kOutput, calls=%fused_computation.20 | convolution fusion | flops 1635778560 | bytes 17776640 | tf_op jit(solution)/shard_map/tsmcf,tsmcd->mfd/dot_general | solution.py:68
  544.2 12.4 %fusion.10 = f32[5,1536,128]{2,1,0:T(8,128)} fusion(bf16[4,8,5,26,1536]{4,1,0,3,2:T(8,128)(2,1)S(1)} %bitcast.163, bf16[4,8,5,26,128]{4,3,1,0,2:T(8,128)(2,1)S(1)} %copy-done.15), kind=kOutput, calls=%fused_computation.19 | convolution fusion | flops 1635778560 | bytes 17776640 | tf_op jit(solution)/shard_map/tsmcd,tsmcf->mdf/dot_general | solution.py:72
  556.6 77.8 %reduce-scatter.5.cloned.1.call-done = bf16[1,8,5,26,1536]{4,1,3,2,0:T(8,128)(2,1)} async-done(((bf16[4,8,5,26,1536]{4,1,3,2,0:T(8,128)(2,1)}), bf16[1,8,5,26,1536]{4,1,3,2,0:T(8,128)(2,1)}) %reduce-scatter.5.cloned.1.call-update) | async-done | bytes 3194896 | tf_op jit(solution)/shard_map/reduce_scatter | solution.py:74
  634.3 4.9 copy.94
  639.2 5.5 all-to-all-start.3
  644.7 17.1 %fusion.7 = f32[5,1536,128]{2,1,0:T(8,128)} fusion(bf16[4,8,5,26,1536]{4,1,0,3,2:T(8,128)(2,1)} %bitcast.160, bf16[4,8,5,26,128]{4,3,1,0,2:T(8,128)(2,1)S(1)} %copy-done.13), kind=kOutput, calls=%fused_computation.18 | convolution fusion | flops 1635778560 | bytes 17776640 | tf_op jit(solution)/shard_map/tsmcd,tsmcf->mdf/dot_general | solution.py:71
  661.8 5.6 reshape.358
  667.4 6.0 gather_fusion.2
  673.4 1.9 fusion.17
  675.5 0.9 fusion.62
  676.4 14.4 %all-to-all-done.3 = bf16[8,5,26,1536]{3,2,1,0:T(8,128)(2,1)} async-done(((bf16[8,5,26,1536]{3,2,1,0:T(8,128)(2,1)}), bf16[8,5,26,1536]{3,2,1,0:T(8,128)(2,1)}, u32[]{:S(2)}, u32[]{:S(2)}) %all-to-all-start.3) | async-done | bytes 3194912 | tf_op jit(solution)/shard_map/all_to_all | solution.py:75
  690.7 5.7 reshape.361
  696.4 6.3 gather_fusion.4
  702.8 1.0 convert_reduce_fusion
  703.9 1.4 fusion.51
  705.3 1.7 convert_reduce_fusion.1
  707.0 43.9 %all-reduce = (f32[1536]{0:T(1024)}, f32[1536]{0:T(1024)}) all-reduce(f32[1536]{0:T(1024)S(1)} %get-tuple-element.14, f32[1536]{0:T(1024)S(1)} %get-tuple-element.56), channel_id=1, replica_groups=mesh['dp'=1,'tp'=4,'ep'=8] {'ep','tp'}, use_global_device_ids=true, to_apply=%region_17.18 | all-reduce | flops 3072 | bytes 24576 | tf_op jit(solution)/shard_map/psum | solution.py:84
  750.9 19.6 %all-reduce.3.cloned.1.call-done = f32[1536,40]{0,1:T(8,128)} async-done(((f32[1536,40]{0,1:T(8,128)}), f32[1536,40]{0,1:T(8,128)}) %all-reduce.3.cloned.1.call-update) | async-done | bytes 245776 | tf_op jit(solution)/shard_map/psum | solution.py:84
  770.5 1.7 copy.131
  (122 shorter events, 2.5 us)
Async XLA Ops:
  7.2 360.2 %copy-start = (bf16[5,128,1536]{2,1,0:T(8,128)(2,1)S(1)}, bf16[5,128,1536]{2,1,0:T(8,128)(2,1)}, u32[]{:S(2)}) copy-start(bf16[5,128,1536]{2,1,0:T(8,128)(2,1)} %param.15) | copy-start | bytes 5898244
  7.2 224.2 %all-gather.5.cloned.1.call-start = ((), (), s32[]{:S(2)}) async-start(), calls=%async_computation.9 | async-start | bytes 15974400 | tf_op jit(solution)/shard_map/all_gather | solution.py:48
  8.5 13.5 %copy-start.32 = (f32[64]{0:T(128)}, f32[64]{0:T(128)S(1)}, u32[]{:S(2)}) copy-start(f32[64]{0:T(128)S(1)} %add_rsqrt_fusion) | copy-start | bytes 772
  9.2 12.8 %copy-start.23 = (f32[1536]{0:T(1024)}, f32[1536]{0:T(1024)S(1)}, u32[]{:S(2)}) copy-start(f32[1536]{0:T(1024)S(1)} %convert_element_type.59) | copy-start | bytes 18436
  14.6 7.4 copy-start.10
  14.6 7.5 copy-start.18
  14.6 7.7 copy-start.26
  14.6 8.5 %copy-start.16 = (bf16[64,1536]{1,0:T(8,128)(2,1)S(1)}, bf16[64,1536]{1,0:T(8,128)(2,1)}, u32[]{:S(2)}) copy-start(bf16[64,1536]{1,0:T(8,128)(2,1)} %param.17) | copy-start | bytes 589828
  22.1 18.9 %copy-start.2 = (bf16[64,1536]{1,0:T(8,128)(2,1)}, bf16[64,1536]{1,0:T(8,128)(2,1)S(1)}, u32[]{:S(2)}) copy-start(bf16[64,1536]{1,0:T(8,128)(2,1)S(1)} %fusion.45) | copy-start | bytes 589828
  22.4 0.6 copy-start.21
  22.4 13.2 %copy-start.28 = (f32[64]{0:T(128)}, f32[64]{0:T(128)S(1)}, u32[]{:S(2)}) copy-start(f32[64]{0:T(128)S(1)} %reduce_max.9) | copy-start | bytes 772
  23.0 12.6 %copy-start.30 = (f32[64]{0:T(128)}, f32[64]{0:T(128)S(1)}, u32[]{:S(2)}) copy-start(f32[64]{0:T(128)S(1)} %fusion.57) | copy-start | bytes 772
  23.1 12.5 %copy-start.19 = (f32[64,8]{1,0:T(8,128)}, f32[64,8]{1,0:T(8,128)S(1)}, u32[]{:S(2)}) copy-start(f32[64,8]{1,0:T(8,128)S(1)} %copy.82) | copy-start | bytes 6148
  23.2 0.7 copy-start.8
  111.7 241.0 %all-gather.7.cloned.1.call-start = ((), (), s32[]{:S(2)}) async-start(), calls=%async_computation.10 | async-start | bytes 15974400 | tf_op jit(solution)/shard_map/all_gather | solution.py:66
  165.8 353.0 %reduce-scatter.3.cloned.1.call-start = ((), (), s32[]{:S(2)}) async-start(), calls=%async_computation.6 | async-start | bytes 15974400 | tf_op jit(solution)/shard_map/reduce_scatter | solution.py:55
  231.4 14.7 %copy-start.6 = (bf16[5,1536,128]{2,1,0:T(8,128)(2,1)S(1)}, bf16[5,1536,128]{2,1,0:T(8,128)(2,1)}, u32[]{:S(2)}) copy-start(bf16[5,1536,128]{2,1,0:T(8,128)(2,1)} %param.14) | copy-start | bytes 5898244
  246.1 9.3 %copy-start.4 = (bf16[5,1536,128]{2,1,0:T(8,128)(2,1)S(1)}, bf16[5,1536,128]{2,1,0:T(8,128)(2,1)}, u32[]{:S(2)}) copy-start(bf16[5,1536,128]{2,1,0:T(8,128)(2,1)} %param.13) | copy-start | bytes 5898244
  404.0 1.5 copy-start.5
  404.0 230.3 %reduce-scatter.5.cloned.1.call-start = ((), (), s32[]{:S(2)}) async-start(), calls=%async_computation.7 | async-start | bytes 15974400 | tf_op jit(solution)/shard_map/reduce_scatter | solution.py:74
  405.5 14.0 %copy-start.7 = (bf16[5,1536,128]{2,1,0:T(8,128)(2,1)S(1)}, bf16[5,1536,128]{2,1,0:T(8,128)(2,1)}, u32[]{:S(2)}) copy-start(bf16[5,1536,128]{2,1,0:T(8,128)(2,1)} %param.14) | copy-start | bytes 5898244
  405.5 14.0 %copy-start.14 = (bf16[4,8,5,26,128]{4,3,1,0,2:T(8,128)(2,1)S(1)}, bf16[4,8,5,26,128]{4,3,1,0,2:T(8,128)(2,1)}, u32[]{:S(2)}) copy-start(bf16[4,8,5,26,128]{4,3,1,0,2:T(8,128)(2,1)} %get-tuple-element.53) | copy-start | bytes 3194884
  452.7 0.7 copy-start.34
  523.7 20.4 %slice-start = ((s8[12779520]{0:T(1024)(128)(4,1)}), s8[196608]{0:T(1024)(128)(4,1)S(1)}, s32[]{:S(2)}) async-start(s8[12779520]{0:T(1024)(128)(4,1)} %bitcast.161), calls=%async_computation.11 | async-start | bytes 393216
  523.7 115.5 %all-to-all-start.1 = ((bf16[8,5,26,1536]{3,2,1,0:T(8,128)(2,1)}), bf16[8,5,26,1536]{3,2,1,0:T(8,128)(2,1)}, u32[]{:S(2)}, u32[]{:S(2)}) async-start(bf16[8,5,26,1536]{3,2,1,0:T(8,128)(2,1)} %copy.88), calls=%async_computation.2 | async-start | bytes 7864320 | tf_op jit(solution)/shard_map/all_to_all | solution.py:56
  529.3 14.8 %slice-start.1 = ((s8[12779520]{0:T(1024)(128)(4,1)}), s8[4194304]{0:T(1024)(128)(4,1)S(1)}, s32[]{:S(2)}) async-start(s8[12779520]{0:T(1024)(128)(4,1)} %bitcast.161), calls=%async_computation.12 | async-start | bytes 8388608
  529.4 14.8 %slice-start.2 = ((s8[12779520]{0:T(1024)(128)(4,1)}), s8[4194304]{0:T(1024)(128)(4,1)S(1)}, s32[]{:S(2)}) async-start(s8[12779520]{0:T(1024)(128)(4,1)} %bitcast.161), calls=%async_computation.13 | async-start | bytes 8388608
  529.4 14.8 %slice-start.3 = ((s8[12779520]{0:T(1024)(128)(4,1)}), s8[4194304]{0:T(1024)(128)(4,1)S(1)}, s32[]{:S(2)}) async-start(s8[12779520]{0:T(1024)(128)(4,1)} %bitcast.161), calls=%async_computation.14 | async-start | bytes 8388608
  529.4 14.8 %copy-start.15 = (bf16[4,8,5,26,128]{4,3,1,0,2:T(8,128)(2,1)S(1)}, bf16[4,8,5,26,128]{4,3,1,0,2:T(8,128)(2,1)}, u32[]{:S(2)}) copy-start(bf16[4,8,5,26,128]{4,3,1,0,2:T(8,128)(2,1)} %get-tuple-element.53) | copy-start | bytes 3194884
  639.2 5.5 copy-start.13
  639.2 51.5 %all-to-all-start.3 = ((bf16[8,5,26,1536]{3,2,1,0:T(8,128)(2,1)}), bf16[8,5,26,1536]{3,2,1,0:T(8,128)(2,1)}, u32[]{:S(2)}, u32[]{:S(2)}) async-start(bf16[8,5,26,1536]{3,2,1,0:T(8,128)(2,1)} %copy.94), calls=%async_computation.5 | async-start | bytes 7864320 | tf_op jit(solution)/shard_map/all_to_all | solution.py:75
  644.7 125.8 %all-reduce.3.cloned.1.call-start = ((), (), s32[]{:S(2)}) async-start(), calls=%async_computation.8 | async-start | bytes 491520 | tf_op jit(solution)/shard_map/psum | solution.py:84
  667.3 6.0 copy-start.9
  667.3 6.0 copy-start.20
  667.3 8.0 %copy-start.22 = (f32[64,8]{0,1:T(8,128)S(1)}, f32[64,8]{0,1:T(8,128)}, u32[]{:S(2)}) copy-start(f32[64,8]{0,1:T(8,128)} %copy-done.21) | copy-start | bytes 6148
  667.3 8.0 %copy-start.29 = (f32[64]{0:T(128)S(1)}, f32[64]{0:T(128)}, u32[]{:S(2)}) copy-start(f32[64]{0:T(128)} %copy-done.28) | copy-start | bytes 772
  667.3 8.0 %copy-start.31 = (f32[64]{0:T(128)S(1)}, f32[64]{0:T(128)}, u32[]{:S(2)}) copy-start(f32[64]{0:T(128)} %copy-done.30) | copy-start | bytes 772
  667.4 8.0 %copy-start.27 = (s32[64,8]{0,1:T(8,128)S(1)}, s32[64,8]{0,1:T(8,128)}, u32[]{:S(2)}) copy-start(s32[64,8]{0,1:T(8,128)} %param.12) | copy-start | bytes 6148
  667.4 8.1 %copy-start.3 = (bf16[64,1536]{1,0:T(8,128)(2,1)S(1)}, bf16[64,1536]{1,0:T(8,128)(2,1)}, u32[]{:S(2)}) copy-start(bf16[64,1536]{1,0:T(8,128)(2,1)} %copy-done.2) | copy-start | bytes 589828
  675.5 15.3 %copy-start.25 = (bf16[64,40]{0,1:T(8,128)(2,1)}, bf16[64,40]{0,1:T(8,128)(2,1)S(1)}, u32[]{:S(2)}) copy-start(bf16[64,40]{0,1:T(8,128)(2,1)S(1)} %select_reduce_fusion) | copy-start | bytes 15364
  696.4 7.4 copy-start.24
  696.4 7.5 copy-start.33
  696.4 75.7 %copy-start.1 = (bf16[5,128,1536]{2,1,0:T(8,128)(2,1)S(1)}, bf16[5,128,1536]{2,1,0:T(8,128)(2,1)}, u32[]{:S(2)}) copy-start(bf16[5,128,1536]{2,1,0:T(8,128)(2,1)} %param.15) | copy-start | bytes 5898244
  702.8 2.5 copy-start.11
  702.8 2.5 copy-start.12
  702.8 2.5 copy-start.17
Sparse Core Ops, SparseCore 0:
  111.9 119.4 all-gather.4
  233.5 119.1 all-gather.6
  404.1 114.5 reduce-scatter.2
  521.0 113.2 reduce-scatter.4
  676.5 93.9 all-reduce.2
where the time goes:
time: 789 us; the launch traced here: 779 us
  waiting for transfers between devices  299 us (38%)
  blocking collectives  146 us (19%)
  local copies, waits for them, and re-layouts  143 us (18%)
  matrix products  118 us (15%)
  other arithmetic  47.1 us (6%)
  between operations  14.9 us (2%)
  starting transfers between devices  11.6 us (1%)
    all_gather x1, waiting for transfers between devices, device_step(): d_rows = lax.all_gather(d_recv, 'tp', axis=0)  88.1 us
    reduce_scatter x1, waiting for transfers between devices, device_step(): lax.psum_scatter(dh_part, 'tp', scatter_dimension=0, tiled=True)[0]  77.8 us
    all_gather x1, waiting for transfers between devices, device_step(): rows_in = lax.all_gather(recv_rows, 'tp', axis=0)  65.3 us
    all_to_all x1, blocking collectives, device_step(): recv_rows = lax.all_to_all(send_rows, 'ep', 0, 0, tiled=True)  51.6 us
    all_to_all x1, blocking collectives, device_step(): d_recv = lax.all_to_all(d_send, 'ep', 0, 0, tiled=True)  50.4 us
    psum x1, blocking collectives, device_step(): lax.psum((d_gain, d_router, d_bias), ('ep', 'tp'))  43.9 us
    reduce_scatter x1, waiting for transfers between devices, device_step(): lax.psum_scatter(part_out, 'tp', scatter_dimension=0, tiled=True)[0]  33.4 us
    sub x1, other arithmetic, routing_tables(): copy_pos = flat_ids * capacity + jnp.argsort(order) - starts[flat_ids]  20.7 us
  transfers between devices with their start and end apart: 7, of which 6 were waited for; matrix products, arithmetic and copies ran while one was open for 26% of the time, Pallas kernels for 0%

commit v1 on v0

v1 whole, which is shorter than its diff:
```python
import jax
import jax.numpy as jnp
from jax import lax
from jax.sharding import PartitionSpec as P

EPS = 1e-6


def solution(mesh):
    tok_spec = P(("dp", "ep", "tp"), None)
    wide_spec = P("ep", None, "tp")
    down_spec = P("ep", "tp", None)
    grad_wide = P(("dp", "ep"), None, "tp")
    grad_down = P(("dp", "ep"), "tp", None)
    group = ("ep", "tp")

    def device_step(x_in, norm_gain, w_router, expert_idx, w_gate, w_up, w_down, out_bias, dy_out):
        n_exp = w_router.shape[1]
        local_exp = w_gate.shape[0]
        x_f32 = x_in.astype(jnp.float32)
        inv_rms = lax.rsqrt(jnp.mean(x_f32 * x_f32, axis=-1, keepdims=True) + EPS)
        normed = x_f32 * inv_rms
        gain_f32 = norm_gain.astype(jnp.float32)
        hidden = (normed * gain_f32).astype(jnp.bfloat16)
        logits = jnp.dot(hidden, w_router, preferred_element_type=jnp.float32)
        chosen = expert_idx[:, :, None] == jnp.arange(n_exp)[None, None, :]
        mask = jnp.any(chosen, axis=1)
        top = jnp.max(jnp.where(mask, logits, -jnp.inf), axis=-1, keepdims=True)
        unnorm = jnp.where(mask, jnp.exp(jnp.minimum(logits - top, 0.0)), 0.0)
        gates = unnorm / jnp.sum(unnorm, axis=-1, keepdims=True)
        all_h = lax.all_gather(hidden, group, axis=0, tiled=True)
        all_g = lax.all_gather(gates, group, axis=0, tiled=True)
        all_dy = lax.all_gather(dy_out, group, axis=0, tiled=True)
        my_g = lax.dynamic_slice_in_dim(all_g, lax.axis_index("ep") * local_exp, local_exp, axis=1)
        gate_pre = jnp.einsum("td,mdf->tmf", all_h, w_gate, preferred_element_type=jnp.float32)
        up_pre = jnp.einsum("td,mdf->tmf", all_h, w_up, preferred_element_type=jnp.float32)
        sigma = jax.nn.sigmoid(gate_pre)
        silu = gate_pre * sigma
        act = silu * up_pre
        gated = (act * my_g[:, :, None]).astype(jnp.bfloat16)
        part_out = jnp.einsum("tmf,mfd->td", gated, w_down, preferred_element_type=jnp.float32).astype(jnp.bfloat16)
        y_sum = lax.psum_scatter(part_out, group, scatter_dimension=0, tiled=True)
        y_out = (x_f32 + y_sum.astype(jnp.float32) + out_bias.astype(jnp.float32)).astype(jnp.bfloat16)
        d_act = jnp.einsum("td,mfd->tmf", all_dy, w_down, preferred_element_type=jnp.float32)
        d_gate_part = jnp.sum(act * d_act, axis=-1)
        d_act = d_act * my_g[:, :, None]
        d_gate_pre = (d_act * up_pre * sigma * (1.0 + gate_pre * (1.0 - sigma))).astype(jnp.bfloat16)
        d_up_pre = (d_act * silu).astype(jnp.bfloat16)
        dh_part = (jnp.einsum("tmf,mdf->td", d_gate_pre, w_gate, preferred_element_type=jnp.float32) + jnp.einsum("tmf,mdf->td", d_up_pre, w_up, preferred_element_type=jnp.float32)).astype(jnp.bfloat16)
        dh_expert = lax.psum_scatter(dh_part, group, scatter_dimension=0, tiled=True).astype(jnp.float32)
        d_gate = jnp.einsum("td,tmf->mdf", all_h, d_gate_pre, preferred_element_type=jnp.float32)
        d_up = jnp.einsum("td,tmf->mdf", all_h, d_up_pre, preferred_element_type=jnp.float32)
        d_down = jnp.einsum("tmf,td->mfd", gated, all_dy, preferred_element_type=jnp.float32)
        d_bias = jnp.sum(all_dy.astype(jnp.float32), axis=0)
        d_gates = lax.all_gather(lax.psum(d_gate_part, "tp"), "ep", axis=1, tiled=True)
        d_logits = all_g * (d_gates - jnp.sum(all_g * d_gates, axis=-1, keepdims=True))
        d_router = jnp.einsum("td,te->de", all_h, d_logits.astype(jnp.bfloat16), preferred_element_type=jnp.float32)
        my = lax.axis_index("ep") * lax.axis_size("tp") + lax.axis_index("tp")
        my_dl = lax.dynamic_slice_in_dim(d_logits, my * x_in.shape[0], x_in.shape[0], axis=0)
        dh_total = dh_expert + jnp.einsum("te,de->td", my_dl, w_router, preferred_element_type=jnp.float32)
        d_gain = lax.psum(jnp.sum(dh_total * normed, axis=0), group)
        d_norm = dh_total * gain_f32
        dy_f32 = dy_out.astype(jnp.float32)
        dx_in = (dy_f32 + inv_rms * (d_norm - normed * jnp.mean(d_norm * normed, axis=-1, keepdims=True))).astype(jnp.bfloat16)
        return y_out, dx_in, d_gain, d_router, d_gate, d_up, d_down, d_bias

    return jax.shard_map(device_step, mesh=mesh, in_specs=(tok_spec, P(None), P(None, None), tok_spec, wide_spec, wide_spec, down_spec, P(None), tok_spec), out_specs=(tok_spec, tok_spec, P("dp"), P("dp", None), grad_wide, grad_wide, grad_down, P("dp")), check_vma=False)
```

time: 789 us -> 297 us (0.38); the launches traced: 779 us -> 296 us
  waiting for transfers between devices: 299 us -> 50.9 us
  local copies, waits for them, and re-layouts: 143 us -> 20 us
  other arithmetic: 47.1 us -> 10.8 us
  matrix products: 118 us -> 82.7 us
  blocking collectives: 146 us -> 118 us
  starting transfers between devices: 11.6 us -> 0.25 us
    all_gather x2, waiting for transfers between devices: 153 us -> 33.4 us  [the longest x1 28.9 us: device_step(): all_dy = lax.all_gather(dy_out, group, axis=0, tiled=True)]
    all_to_all x2 -> x0, blocking collectives: 102 us -> none  [the longest x1 51.6 us: device_step(): recv_rows = lax.all_to_all(send_rows, 'ep', 0, 0, tiled=True)]
    reduce_scatter x2, waiting for transfers between devices: 111 us -> 16.6 us  [the longest x1 16.6 us: device_step(): y_sum = lax.psum_scatter(part_out, group, scatter_dimension=0, tiled=True)]
    all_gather x0 -> x2, blocking collectives: none -> 54.5 us  [the longest x1 34 us: device_step(): all_g = lax.all_gather(gates, group, axis=0, tiled=True)]
    dot_general x11 -> x9, matrix products: 118 us -> 65.5 us  [the longest x1 12.3 us: device_step(): jnp.einsum('td,mfd->tmf', all_dy, w_down, preferred_element_type=jnp.floa...]
    gather x11 -> x0, local copies, waits for them, and re-layouts: 47.7 us -> none  [the longest x2 15.7 us: device_step(): dy_copy[slot_copy]]
    convert_element_type x2 -> x0, local copies, waits for them, and re-layouts: 30.9 us -> none  [the longest x1 15.7 us: device_step(): jnp.einsum('tsmcf,mfd->tsmcd', hidden_act, w_down, preferred_element_type...]
    all_gather x2 -> x1, local copies, waits for them, and re-layouts: 29.3 us -> 0.13 us  [device_step(): all_g = lax.all_gather(gates, group, axis=0, tiled=True)]
  transfers between devices with their start and end apart: 7 -> 4, of which waited for: 6 -> 3; matrix products, arithmetic and copies ran while one was open for 26% -> 28% of each run, Pallas kernels for 0% -> 0%
where the time goes in v1:
time: 297 us; the launch traced here: 296 us
  blocking collectives  118 us (40%)
  matrix products  82.7 us (28%)
  waiting for transfers between devices  50.9 us (17%)
  local copies, waits for them, and re-layouts  20 us (7%)
  between operations  14 us (5%)
  other arithmetic  10.8 us (4%)
    psum x1, blocking collectives, device_step(): d_gain = lax.psum(jnp.sum(dh_total * normed, axis=0), group)  50.7 us
    all_gather x1, blocking collectives, device_step(): all_g = lax.all_gather(gates, group, axis=0, tiled=True)  34 us
    all_gather x1, waiting for transfers between devices, device_step(): all_dy = lax.all_gather(dy_out, group, axis=0, tiled=True)  28.9 us
    all_gather x1, blocking collectives, device_step(): lax.all_gather(lax.psum(d_gate_part, 'tp'), 'ep', axis=1, tiled=True)  20.5 us
    unnamed x36, local copies, waits for them, and re-layouts  19.8 us
    reduce_scatter x1, waiting for transfers between devices, device_step(): y_sum = lax.psum_scatter(part_out, group, scatter_dimension=0, tiled=True)  16.6 us
    unnamed x2, matrix products  16 us
    psum x1, blocking collectives, device_step(): lax.psum(d_gate_part, 'tp')  12.5 us
  transfers between devices with their start and end apart: 4, of which 3 were waited for; matrix products, arithmetic and copies ran while one was open for 28% of the time, Pallas kernels for 0%

profile of v1, /device:TPU:97, one launch (start us, length us, event | category | flops | bytes accessed | tf_op | source)
XLA Modules:
  0.0 296.3 jit_solution(1296645815094785638)
XLA Ops:
  7.2 0.0 copy-start
  7.2 0.1 all-gather.5.cloned.1.call-start
  7.3 1.2 fusion.27
  8.5 0.7 convert_element_type.49
  9.2 1.7 fusion.20
  10.9 0.1 all-gather.5.cloned.1.call-update
  11.0 0.1 all-gather.7.cloned.1.call-start
  11.0 0.7 all-gather.7.cloned.1.call-update
  11.8 0.1 reduce-scatter.5.cloned.1.call-start
  11.8 0.7 fusion.34
  12.6 1.2 select_reduce_fusion
  13.8 34.0 %all-gather = f32[32,64,40]{1,2,0:T(8,128)S(1)} all-gather(f32[1,64,40]{1,2,0:T(8,128)S(1)} %divide_bitcast_fusion), channel_id=1, replica_groups=mesh['dp'=1,'tp'=4,'ep'=8] {'ep','tp'}, dimensions={0}, use_global_device_ids=true | all-gather | bytes 337920 | tf_op jit(solution)/shard_map/all_gather | solution.py:32
  47.8 0.1 copy.45
  47.9 0.2 reshape.36
  48.2 4.0 %copy.43 = bf16[5,1536,128]{1,2,0:T(8,128)(2,1)} copy(bf16[5,1536,128]{2,1,0:T(8,128)(2,1)} %param.13) | data formatting | bytes 3932160 | tf_op args[4]
  52.2 4.0 %copy.44 = bf16[5,1536,128]{1,2,0:T(8,128)(2,1)} copy(bf16[5,1536,128]{2,1,0:T(8,128)(2,1)} %param.14) | data formatting | bytes 3932160 | tf_op args[5]
  56.2 4.5 %all-gather.5.cloned.1.call-done = bf16[2048,1536]{1,0:T(8,128)(2,1)} async-done(((bf16[64,1536]{1,0:T(8,128)(2,1)}), bf16[2048,1536]{1,0:T(8,128)(2,1)}) %all-gather.5.cloned.1.call-update) | async-done | bytes 6291472 | tf_op jit(solution)/shard_map/all_gather | solution.py:31
  60.7 0.0 copy-start.2
  60.7 10.0 %fusion.39 = f32[2048,640]{0,1} fusion(bf16[2048,1536]{1,0:T(8,128)(2,1)} %all-gather.5.cloned.1.call-done, bf16[1536,640]{0,1:T(8,128)(2,1)} %bitcast.72), kind=kOutput, calls=%fused_computation.56 | convolution fusion | flops 4026531840 | bytes 13500416
  70.7 0.0 copy-done.2
  70.7 0.0 copy-done.6
  70.7 6.0 %fusion.38 = f32[2048,640]{0,1} fusion(bf16[2048,1536]{1,0:T(8,128)(2,1)S(1)} %copy-done.2, bf16[1536,640]{0,1:T(8,128)(2,1)S(1)} %bitcast.71), kind=kOutput, calls=%fused_computation.55 | convolution fusion | flops 4026531840 | bytes 13500416
  76.7 28.9 %all-gather.7.cloned.1.call-done = bf16[2048,1536]{1,0:T(8,128)(2,1)} async-done(((bf16[64,1536]{1,0:T(8,128)(2,1)}), bf16[2048,1536]{1,0:T(8,128)(2,1)}) %all-gather.7.cloned.1.call-update) | async-done | bytes 6291472 | tf_op jit(solution)/shard_map/all_gather | solution.py:33
  105.6 0.0 copy-done
  105.6 12.3 %multiply_reduce_fusion = (f32[2048,5]{0,1:T(8,128)S(1)}, bf16[2048,5,128]{0,2,1:T(8,128)(2,1)S(1)}, bf16[2048,5,128]{0,2,1:T(8,128)(2,1)}, bf16[2048,5,128]{0,2,1:T(8,128)(2,1)S(1)}) fusion(f32[2048,5,128]{0,2,1:T(8,128)} %bitcast.74, f32[2048,5,128]{0,2,1:T(8,128)} %bitcast.75, f32[2048,5]{0,1:T(8,128)S(1)} %constant_dynamic-slice_fusion, ...), kind=kOutput, calls=%fused_computation.12 | convolution fusion | flops 4051425280 | bytes 26689536 | tf_op jit(solution)/shard_map/td,mfd->tmf/dot_general | solution.py:44
  117.8 0.0 copy-done.4
  117.8 0.0 copy-start.5
  117.8 5.1 %fusion.40 = f32[2048,1536,1]{1,0,2:T(8,128)S(1)} fusion(bf16[2048,5,128]{0,2,1:T(8,128)(2,1)S(1)} %get-tuple-element.43, bf16[5,1536,128]{2,1,0:T(8,128)(2,1)S(1)} %copy-done.4), kind=kOutput, calls=%fused_computation.57 | convolution fusion | flops 4026531840 | bytes 17170432 | tf_op jit(solution)/shard_map/tmf,mdf->td/dot_general | solution.py:49
  123.0 0.0 copy-done.10
  123.0 0.0 copy-done.11
  123.0 0.0 copy-done.5
  123.0 7.4 %fusion = bf16[2048,1536]{1,0:T(8,128)(2,1)} fusion(f32[2048,1536,1]{1,0,2:T(8,128)S(1)} %fusion.40, bf16[2048,5,128]{0,2,1:T(8,128)(2,1)S(1)} %get-tuple-element.45, bf16[5,1536,128]{2,1,0:T(8,128)(2,1)S(1)} %copy-done.5), kind=kOutput, calls=%fused_computation.1 | convolution fusion | flops 4032823296 | bytes 23461888 | tf_op jit(solution)/shard_map/tmf,mdf->td/dot_general | solution.py:49
  130.5 0.1 reduce-scatter.5.cloned.1.call-update
  130.5 0.1 reduce-scatter.3.cloned.1.call-start
  130.6 8.9 %bitcast_convert_fusion = bf16[2048,1536]{1,0:T(8,128)(2,1)} fusion(bf16[2048,5,128]{0,2,1:T(8,128)(2,1)} %get-tuple-element.44, bf16[5,128,1536]{2,1,0:T(8,128)(2,1)S(1)} %copy-done), kind=kOutput, calls=%fused_computation.2 | convolution fusion | flops 4029677568 | bytes 10878976 | tf_op jit(solution)/shard_map/tmf,mfd->td/dot_general | solution.py:41
  139.6 0.1 reduce-scatter.3.cloned.1.call-update
  139.6 0.6 copy-done.9
  140.2 12.5 %psum.14 = f32[2048,5]{0,1:T(8,128)S(1)} all-reduce(f32[2048,5]{0,1:T(8,128)S(1)} %get-tuple-element.42), channel_id=1, replica_groups=mesh['dp'=1,'tp'=4,'ep'=8] {'tp'}, use_global_device_ids=true, to_apply=%region_7.8 | all-reduce | flops 10240 | bytes 81920 | tf_op jit(solution)/shard_map/psum | solution.py:55
  152.7 20.5 %all-gather.1 = f32[8,5,2048]{2,1,0:T(8,128)S(1)} all-gather(f32[1,5,2048]{2,1,0:T(8,128)S(1)} %bitcast.73), channel_id=1, replica_groups=mesh['dp'=1,'tp'=4,'ep'=8] {'ep'}, dimensions={0}, use_global_device_ids=true | all-gather | bytes 368640 | tf_op jit(solution)/shard_map/all_gather | solution.py:55
  173.2 0.1 reshape.38
  173.3 9.7 %fusion.13 = f32[5,1536,128]{1,2,0:T(8,128)} fusion(bf16[2048,5,128]{0,2,1:T(8,128)(2,1)} %copy-done.11, bf16[2048,1536]{1,0:T(8,128)(2,1)} %all-gather.5.cloned.1.call-done), kind=kOutput, calls=%fused_computation.19 | convolution fusion | flops 4026531840 | bytes 12845056 | tf_op jit(solution)/shard_map/td,tmf->mdf/dot_general | solution.py:52
  183.0 5.4 %copy.50 = f32[5,1536,128]{2,1,0:T(8,128)} copy(f32[5,1536,128]{1,2,0:T(8,128)} %fusion.13) | data formatting | bytes 7864320
  188.5 9.7 %fusion.10 = f32[5,1536,128]{1,2,0:T(8,128)} fusion(bf16[2048,5,128]{0,2,1:T(8,128)(2,1)} %copy-done.10, bf16[2048,1536]{1,0:T(8,128)(2,1)} %all-gather.5.cloned.1.call-done), kind=kOutput, calls=%fused_computation.18 | convolution fusion | flops 4026531840 | bytes 12845056 | tf_op jit(solution)/shard_map/td,tmf->mdf/dot_general | solution.py:51
  198.2 5.4 %copy.49 = f32[5,1536,128]{2,1,0:T(8,128)} copy(f32[5,1536,128]{1,2,0:T(8,128)} %fusion.10) | data formatting | bytes 7864320
  203.7 0.0 slice-start
  203.7 4.5 %convert_reduce_fusion = f32[1536]{0:T(1024)} fusion(bf16[2048,1536]{1,0:T(8,128)(2,1)} %all-gather.7.cloned.1.call-done), kind=kLoop, calls=%fused_computation.3 | loop fusion | flops 6289920 | bytes 6297600 | tf_op jit(solution)/shard_map/reduce_sum | solution.py:54
  208.2 0.0 slice-start.1
  208.2 4.8 %fusion.41 = f32[1536,40]{0,1:T(8,128)} fusion(bf16[2048,1536]{1,0:T(8,128)(2,1)} %all-gather.5.cloned.1.call-done, bf16[2048,40]{0,1:T(8,128)(2,1)S(1)} %fusion.31), kind=kOutput, calls=%fused_computation.58 | convolution fusion | flops 251658240 | bytes 6701056 | tf_op jit(solution)/shard_map/td,te->de/dot_general | solution.py:57
  213.0 0.0 slice-done
  213.0 0.0 copy-done.12
  213.0 0.0 slice-done.1
  213.0 0.0 copy-start.3
  213.0 0.0 copy-start.8
  213.0 0.0 copy-start.7
  213.0 0.0 copy-start.1
  213.0 6.2 %fusion.5 = f32[5,128,1536]{2,1,0:T(8,128)} fusion(bf16[2048,5,128]{0,2,1:T(8,128)(2,1)S(1)} %copy-done.12, bf16[2048,1536]{1,0:T(8,128)(2,1)S(1)} %bitcast.70), kind=kOutput, calls=%fused_computation.8 | convolution fusion | flops 4026531840 | bytes 12845056 | tf_op jit(solution)/shard_map/tmf,td->mfd/dot_general | solution.py:53
  219.2 0.0 copy-done.3
  219.2 0.0 copy-done.8
  219.2 1.4 fusion.26
  220.6 50.7 %psum.15 = f32[1536]{0:T(1024)} all-reduce(f32[1536]{0:T(1024)S(1)} %get-tuple-element.40), channel_id=1, replica_groups=mesh['dp'=1,'tp'=4,'ep'=8] {'ep','tp'}, use_global_device_ids=true, to_apply=%region_11.12 | all-reduce | flops 1536 | bytes 12288 | tf_op jit(solution)/shard_map/psum | solution.py:61
  271.3 16.6 %reduce-scatter.3.cloned.1.call-done = bf16[64,1536]{1,0:T(8,128)(2,1)} async-done(((bf16[2048,1536]{1,0:T(8,128)(2,1)}), bf16[64,1536]{1,0:T(8,128)(2,1)}) %reduce-scatter.3.cloned.1.call-update) | async-done | bytes 196624 | tf_op jit(solution)/shard_map/reduce_scatter | solution.py:42
  287.9 0.0 copy-done.7
  287.9 1.9 fusion.25
  289.8 0.0 copy-done.1
  (16 shorter events, 0.2 us)
Async XLA Ops:
  7.2 98.4 %copy-start = (bf16[5,128,1536]{2,1,0:T(8,128)(2,1)S(1)}, bf16[5,128,1536]{2,1,0:T(8,128)(2,1)}, u32[]{:S(2)}) copy-start(bf16[5,128,1536]{2,1,0:T(8,128)(2,1)} %param.15) | copy-start | bytes 5898244
  7.2 53.5 %all-gather.5.cloned.1.call-start = ((), (), s32[]{:S(2)}) async-start(), calls=%async_computation.2 | async-start | bytes 6488064 | tf_op jit(solution)/shard_map/all_gather | solution.py:31
  11.0 94.6 %all-gather.7.cloned.1.call-start = ((), (), s32[]{:S(2)}) async-start(), calls=%async_computation.4 | async-start | bytes 6488064 | tf_op jit(solution)/shard_map/all_gather | solution.py:33
  11.8 207.4 %reduce-scatter.5.cloned.1.call-start = ((), (), s32[]{:S(2)}) async-start(), calls=%async_computation.5 | async-start | bytes 6488064 | tf_op jit(solution)/shard_map/reduce_scatter | solution.py:50
  60.7 10.1 %copy-start.2 = (bf16[2048,1536]{1,0:T(8,128)(2,1)S(1)}, bf16[2048,1536]{1,0:T(8,128)(2,1)}, u32[]{:S(2)}) copy-start(bf16[2048,1536]{1,0:T(8,128)(2,1)} %all-gather.5.cloned.1.call-done) | copy-start | bytes 18874372
  60.7 10.1 %copy-start.6 = (bf16[5,1536,128]{1,2,0:T(8,128)(2,1)S(1)}, bf16[5,1536,128]{1,2,0:T(8,128)(2,1)}, u32[]{:S(2)}) copy-start(bf16[5,1536,128]{1,2,0:T(8,128)(2,1)} %copy.43) | copy-start | bytes 5898244
  105.6 12.3 %copy-start.4 = (bf16[5,1536,128]{2,1,0:T(8,128)(2,1)S(1)}, bf16[5,1536,128]{2,1,0:T(8,128)(2,1)}, u32[]{:S(2)}) copy-start(bf16[5,1536,128]{2,1,0:T(8,128)(2,1)} %param.13) | copy-start | bytes 5898244
  117.8 5.2 %copy-start.10 = (bf16[2048,5,128]{0,2,1:T(8,128)(2,1)}, bf16[2048,5,128]{0,2,1:T(8,128)(2,1)S(1)}, u32[]{:S(2)}) copy-start(bf16[2048,5,128]{0,2,1:T(8,128)(2,1)S(1)} %get-tuple-element.43) | copy-start | bytes 7864324
  117.8 5.2 %copy-start.11 = (bf16[2048,5,128]{0,2,1:T(8,128)(2,1)}, bf16[2048,5,128]{0,2,1:T(8,128)(2,1)S(1)}, u32[]{:S(2)}) copy-start(bf16[2048,5,128]{0,2,1:T(8,128)(2,1)S(1)} %get-tuple-element.45) | copy-start | bytes 7864324
  117.8 5.2 %copy-start.5 = (bf16[5,1536,128]{2,1,0:T(8,128)(2,1)S(1)}, bf16[5,1536,128]{2,1,0:T(8,128)(2,1)}, u32[]{:S(2)}) copy-start(bf16[5,1536,128]{2,1,0:T(8,128)(2,1)} %param.14) | copy-start | bytes 5898244
  130.5 157.4 %reduce-scatter.3.cloned.1.call-start = ((), (), s32[]{:S(2)}) async-start(), calls=%async_computation.3 | async-start | bytes 6488064 | tf_op jit(solution)/shard_map/reduce_scatter | solution.py:42
  139.6 0.7 copy-start.9
  203.7 9.3 %slice-start = ((s8[6291456]{0:T(1024)(128)(4,1)}), s8[2097152]{0:T(1024)(128)(4,1)S(1)}, s32[]{:S(2)}) async-start(s8[6291456]{0:T(1024)(128)(4,1)} %bitcast.69), calls=%async_computation.6 | async-start | bytes 4194304
  208.1 4.8 %copy-start.12 = (bf16[2048,5,128]{0,2,1:T(8,128)(2,1)S(1)}, bf16[2048,5,128]{0,2,1:T(8,128)(2,1)}, u32[]{:S(2)}) copy-start(bf16[2048,5,128]{0,2,1:T(8,128)(2,1)} %get-tuple-element.44) | copy-start | bytes 7864324
  208.2 4.8 %slice-start.1 = ((s8[6291456]{0:T(1024)(128)(4,1)}), s8[4194304]{0:T(1024)(128)(4,1)S(1)}, s32[]{:S(2)}) async-start(s8[6291456]{0:T(1024)(128)(4,1)} %bitcast.69), calls=%async_computation.7 | async-start | bytes 8388608
  213.0 6.2 %copy-start.3 = (bf16[64,1536]{1,0:T(8,128)(2,1)S(1)}, bf16[64,1536]{1,0:T(8,128)(2,1)}, u32[]{:S(2)}) copy-start(bf16[64,1536]{1,0:T(8,128)(2,1)} %param.9) | copy-start | bytes 589828
  213.0 6.2 %copy-start.8 = (bf16[1536,40]{0,1:T(8,128)(2,1)S(1)}, bf16[1536,40]{0,1:T(8,128)(2,1)}, u32[]{:S(2)}) copy-start(bf16[1536,40]{0,1:T(8,128)(2,1)} %param.11) | copy-start | bytes 368644
  213.0 74.9 %copy-start.7 = (bf16[64,1536]{1,0:T(8,128)(2,1)S(1)}, bf16[64,1536]{1,0:T(8,128)(2,1)}, u32[]{:S(2)}) copy-start(bf16[64,1536]{1,0:T(8,128)(2,1)} %param.17) | copy-start | bytes 589828
  213.0 76.8 %copy-start.1 = (bf16[5,128,1536]{2,1,0:T(8,128)(2,1)S(1)}, bf16[5,128,1536]{2,1,0:T(8,128)(2,1)}, u32[]{:S(2)}) copy-start(bf16[5,128,1536]{2,1,0:T(8,128)(2,1)} %param.15) | copy-start | bytes 5898244
Sparse Core Ops, SparseCore 0:
  11.1 49.5 all-gather.4
  62.8 42.7 all-gather.6
  130.7 75.4 reduce-scatter.4
  209.6 78.2 reduce-scatter.2

commit v2 on v1

v2 whole, which is shorter than its diff:
```python
import functools

import jax
import jax.numpy as jnp
from jax import lax
from jax.experimental import pallas as pl
from jax.experimental.pallas import tpu as pltpu
from jax.sharding import PartitionSpec as P

EPS = 1e-6
CORES = 2
BF16, F32 = jnp.bfloat16, jnp.float32
MESH = pl.DeviceIdType.MESH
NT = (((1,), (1,)), ((), ()))
TN = (((0,), (0,)), ((), ()))


def rows(start, size):
    return pl.ds(pl.multiple_of(start, size & -size), size)


class Place:
    def __init__(self, side):
        ep = lax.axis_index("ep")
        self.side = side
        self.x, self.c, self.y = lax.div(ep, CORES), lax.rem(ep, CORES), lax.axis_index("tp")

    def along(self, axis, step):
        if axis == "x":
            return {"ep": lax.rem(self.x + step + self.side, self.side) * CORES + self.c, "tp": self.y}
        return {"ep": self.x * CORES + self.c, "tp": lax.rem(self.y + step + self.side, self.side)}

    def partner(self):
        return {"ep": self.x * CORES + 1 - self.c, "tp": self.y}


class Half:
    def __init__(self, place, which, blk):
        self.p, self.which, self.blk, n = place, which, blk, place.side
        self.base = which * n
        self.major, self.minor = ("x", "y") if which == 0 else ("y", "x")
        self.m, self.n = (place.x, place.y) if which == 0 else (place.y, place.x)
        self.span = n * blk

    def tile(self, step):
        return self.base + lax.rem(self.m + step + self.p.side, self.p.side)

    def mine(self, part=0, parts=1):
        size = self.span // parts
        return rows(self.p.c * self.span + part * size, size)

    def block(self, step, part=0, parts=1):
        size = self.blk // parts
        return rows(self.p.c * self.span + lax.rem(self.n + step + self.p.side, self.p.side) * self.blk + part * size, size)


class Gather:
    COPIES = 12

    def __init__(self, halves, own, buf, send, recv):
        self.halves, self.own, self.buf, self.send, self.recv = halves, own, buf, send, recv

    def copy(self, h, k, src, dst, target):
        i = h.which * self.COPIES + k
        return pltpu.make_async_remote_copy(src_ref=src, dst_ref=dst, send_sem=self.send.at[i], recv_sem=self.recv.at[i], device_id=target, device_id_type=MESH)

    def make(self, h, k):
        b, p = self.buf, h.p
        same = lambda t, r, target: self.copy(h, k, b.at[t, r], b.at[t, r], target)
        if k < 2:
            return self.copy(h, k, self.own.at[pl.ds(h.which * h.blk, h.blk)], b.at[h.tile(0), h.block(0)], p.along(h.minor, 1 - 2 * k))
        if k < 4:
            s = 1 - 2 * (k - 2)
            return same(h.tile(0), h.block(-s, k - 2, 2), p.along(h.minor, s))
        if k < 6:
            return same(h.tile(0), h.mine(), p.along(h.major, 1 - 2 * (k - 4)))
        if k < 8:
            s = 1 - 2 * (k - 6)
            return same(h.tile(-s), h.mine(k - 6, 2), p.along(h.major, s))
        return same(h.tile((0, -1, 1, 2)[k - 8]), h.mine(), p.partner())

    def own_copy(self, h, sem):
        return pltpu.make_async_copy(self.own.at[pl.ds(h.which * h.blk, h.blk)], self.buf.at[h.tile(0), h.block(0)], sem)

    def start(self, *ks):
        for k in ks:
            for h in self.halves:
                self.make(h, k).start()

    def wait(self, *ks):
        for k in ks:
            for h in self.halves:
                self.make(h, k).wait_recv()

    def finish(self):
        for k in range(self.COPIES):
            for h in self.halves:
                self.make(h, k).wait_send()

    def begin(self, local):
        self.start(0, 1)
        for h in self.halves:
            self.own_copy(h, local.at[h.which]).start()

    def step(self, k, local=None):
        if k == 0:
            for h in self.halves:
                self.own_copy(h, local.at[h.which]).wait()
            self.wait(0, 1)
            self.start(2, 3)
        elif k == 1:
            self.wait(2, 3)
            self.start(4, 5, 8)
        elif k == 2:
            self.wait(4, 5)
            self.start(6, 7, 9, 10)
        elif k == 3:
            self.wait(6, 7)
            self.start(11)
        elif k == 4:
            self.wait(8)
        elif k == 5:
            self.wait(9, 10)
        else:
            self.wait(11)


class Scatter:
    COPIES = 8

    def __init__(self, halves, part, swap, big, small, out, send, recv, swap_send, swap_recv):
        self.halves, self.part, self.swap, self.big, self.small, self.out = halves, part, swap, big, small, out
        self.send, self.recv, self.swap_send, self.swap_recv = send, recv, swap_send, swap_recv

    def swap_copy(self, t, p, span):
        theirs = rows((1 - p.c) * span, span)
        return pltpu.make_async_remote_copy(src_ref=self.part.at[t, theirs], dst_ref=self.swap.at[t], send_sem=self.swap_send.at[t], recv_sem=self.swap_recv.at[t], device_id=p.partner(), device_id_type=MESH)

    def swapped(self, h, step):
        t = h.tile(step)
        self.swap_copy(t, h.p, h.span).wait_recv()
        self.add(t, h.mine(), self.swap[t])

    def add(self, t, r, *terms):
        total = self.part[t, r].astype(F32)
        for term in terms:
            total = total + term.astype(F32)
        self.part[t, r] = total.astype(BF16)

    def land(self, h, k):
        s, b = h.span, h.blk
        if k < 2:
            return self.big.at[h.which, pl.ds(k * (s // 2), s // 2)]
        if k < 4:
            return self.big.at[h.which, pl.ds(s + (k - 2) * s, s)]
        if k < 6:
            return self.small.at[h.which, pl.ds((k - 4) * (b // 2), b // 2)]
        return self.small.at[h.which, pl.ds(b + (k - 6) * b, b)]

    def make(self, h, k):
        s = 1 - 2 * (k % 2)
        if k < 2:
            src, axis = self.part.at[h.tile(2), h.mine(k, 2)], h.major
        elif k < 4:
            src, axis = self.part.at[h.tile(s), h.mine()], h.major
        elif k < 6:
            src, axis = self.part.at[h.tile(0), h.block(2, k - 4, 2)], h.minor
        else:
            src, axis = self.part.at[h.tile(0), h.block(s)], h.minor
        i = h.which * self.COPIES + k
        return pltpu.make_async_remote_copy(src_ref=src, dst_ref=self.land(h, k), send_sem=self.send.at[i], recv_sem=self.recv.at[i], device_id=h.p.along(axis, s), device_id_type=MESH)

    def step(self, k):
        for h in self.halves:
            if k == 0:
                self.swapped(h, 2)
                self.make(h, 0).start()
                self.make(h, 1).start()
            elif k == 1:
                for q in (1, -1, 0):
                    self.swapped(h, q)
            elif k == 2:
                for d in (0, 1):
                    self.make(h, d).wait_recv()
                    self.add(h.tile(1 - 2 * d), h.mine(d, 2), self.land(h, d)[...])
                    self.make(h, 2 + d).start()
            elif k == 3:
                self.make(h, 2).wait_recv()
                self.make(h, 3).wait_recv()
                self.add(h.tile(0), h.mine(), self.land(h, 2)[...], self.land(h, 3)[...])
                self.make(h, 4).start()
                self.make(h, 5).start()
            elif k == 4:
                for d in (0, 1):
                    self.make(h, 4 + d).wait_recv()
                    self.add(h.tile(0), h.block(1 - 2 * d, d, 2), self.land(h, 4 + d)[...])
                    self.make(h, 6 + d).start()
            elif k == 5:
                self.make(h, 6).wait_recv()
                self.make(h, 7).wait_recv()
                total = self.part[h.tile(0), h.block(0)].astype(F32) + self.land(h, 6)[...].astype(F32) + self.land(h, 7)[...].astype(F32)
                self.out[pl.ds(h.which * h.blk, h.blk)] = total
            else:
                for i in range(self.COPIES):
                    self.make(h, i).wait_send()


def moe_kernel(side, d, e_loc, ff, h_in, dy_in, sel, sel_t, wg_hbm, wu_hbm, wd_hbm,
               y_sum, dh_sum, d_bias, d_router_t, d_logits_t, dwg_hbm, dwu_hbm, dwd_hbm,
               hid, dys, dgs, dg_own, w_gu, w_d, gated, d_gu, part_y, part_dh, swap, big_y, big_dh, small_y, small_dh,
               gu_s, gx_s, da_s, wd_s, bias_s,
               w_sem, local, g_send, g_recv, s_send, s_recv, swap_send, swap_recv, out_sem):
    place = Place(side)
    n_tile = 2 * side
    blk = h_in.shape[0] // 2
    halves = [Half(place, 0, blk), Half(place, 1, blk)]
    tile_rows = hid.shape[1]
    span = tile_rows // CORES

    weights = []
    for e in range(e_loc):
        weights.append(pltpu.make_async_copy(wg_hbm.at[e], w_gu.at[:, pl.ds(2 * e * ff, ff)], w_sem.at[3 * e]))
        weights.append(pltpu.make_async_copy(wu_hbm.at[e], w_gu.at[:, pl.ds((2 * e + 1) * ff, ff)], w_sem.at[3 * e + 1]))
        weights.append(pltpu.make_async_copy(wd_hbm.at[e], w_d.at[pl.ds(e * ff, ff)], w_sem.at[3 * e + 2]))

    barrier = pltpu.get_barrier_semaphore()
    peers = [place.along("x", 1), place.along("x", -1), place.along("y", 1), place.along("y", -1), place.partner()]
    for peer in peers:
        pl.semaphore_signal(barrier, inc=1, device_id=peer, device_id_type=MESH)
    for w in weights:
        w.start()
    pl.semaphore_wait(barrier, len(peers))

    gather_h = Gather(halves, h_in, hid, g_send.at[0], g_recv.at[0])
    gather_dy = Gather(halves, dy_in, dys, g_send.at[1], g_recv.at[1])
    gather_dg = Gather(halves, dg_own, dgs, g_send.at[2], g_recv.at[2])
    scat_y = Scatter(halves, part_y, swap.at[0], big_y, small_y, y_sum, s_send.at[0], s_recv.at[0], swap_send.at[0], swap_recv.at[0])
    scat_dh = Scatter(halves, part_dh, swap.at[1], big_dh, small_dh, dh_sum, s_send.at[1], s_recv.at[1], swap_send.at[1], swap_recv.at[1])

    gather_h.begin(local.at[0])
    gather_dy.begin(local.at[1])
    gather_h.step(0, local.at[0])
    gather_dy.step(0, local.at[1])
    for w in weights:
        w.wait()
    gather_h.step(1)
    gather_dy.step(1)

    lane = lax.broadcasted_iota(jnp.int32, (tile_rows, 128), 1)

    def tile_step(i, _):
        @pl.when(i == 0)
        def _():
            gather_h.step(4)
            gather_dy.step(4)

        @pl.when(i == 2)
        def _():
            gather_h.step(2)
            gather_dy.step(2)
            gather_h.step(5)
            gather_dy.step(5)

        @pl.when(i == 6)
        def _():
            gather_h.step(3)
            gather_dy.step(3)
            gather_h.step(6)
            gather_dy.step(6)

        j, which = lax.div(i, 2), lax.rem(i, 2)
        off = j + lax.div(j, 2) - 2 * lax.div(j, 3)
        t = which * side + lax.rem(place.x * (1 - which) + place.y * which + off, side)
        gu_s[...] = jnp.dot(hid[t, :, pl.ds(0, d)], w_gu[...], preferred_element_type=F32)
        gx_s[...] = jnp.dot(hid[t, :, pl.ds(d, 128)], sel[...], preferred_element_type=F32)
        da_s[...] = lax.dot_general(dys[t], w_d[...], NT, preferred_element_type=F32)
        bias_s[t] = jnp.sum(dys[t].astype(F32), axis=0, keepdims=True)
        sums = jnp.zeros((tile_rows, 128), F32)
        for e in range(e_loc):
            pre, up = gu_s[:, pl.ds(2 * e * ff, ff)], gu_s[:, pl.ds((2 * e + 1) * ff, ff)]
            gate, da = gx_s[:, pl.ds(e * ff, ff)], da_s[:, pl.ds(e * ff, ff)]
            sigma = jax.nn.sigmoid(pre)
            silu = pre * sigma
            act = silu * up
            gated[t, :, pl.ds(e * ff, ff)] = (act * gate).astype(BF16)
            sums = sums + jnp.where(lane == e, jnp.sum(act * da, axis=1, keepdims=True), 0.0)
            da = da * gate
            d_gu[t, :, pl.ds(2 * e * ff, ff)] = (da * up * sigma * (1.0 + pre * (1.0 - sigma))).astype(BF16)
            d_gu[t, :, pl.ds((2 * e + 1) * ff, ff)] = (da * silu).astype(BF16)
        dg_own[rows(t * 8, 8)] = jnp.transpose(sums)[:8]
        part_y[t] = jnp.dot(gated[t], w_d[...], preferred_element_type=F32).astype(BF16)
        scat_y.swap_copy(t, place, span).start()
        part_dh[t] = lax.dot_general(d_gu[t], w_gu[...], NT, preferred_element_type=F32).astype(BF16)
        scat_dh.swap_copy(t, place, span).start()
        return 0

    lax.fori_loop(0, n_tile, tile_step, 0)

    gather_dg.begin(local.at[2])
    d_bias[...] = jnp.sum(bias_s[...], axis=0)
    scat_y.step(0)
    gather_dg.step(0, local.at[2])
    scat_dh.step(0)
    gather_dg.step(1)
    scat_y.step(1)
    scat_dh.step(1)

    m_blk = gu_s.shape[0]
    n_m = d // m_blk

    def wide_copies(mb):
        out = []
        for e in range(e_loc):
            for j, ref in enumerate((dwg_hbm, dwu_hbm)):
                out.append(pltpu.make_async_copy(gu_s.at[:, pl.ds((2 * e + j) * ff, ff)], ref.at[e, rows(mb * m_blk, m_blk)], out_sem.at[2 * e + j]))
        return out

    def wide_step(mb, _):
        @pl.when(mb > 0)
        def _():
            for cp in wide_copies(mb - 1):
                cp.wait()
        a = hid[:, :, rows(mb * m_blk, m_blk)].reshape(n_tile * tile_rows, m_blk)
        b = d_gu[...].reshape(n_tile * tile_rows, 2 * e_loc * ff)
        gu_s[...] = lax.dot_general(a, b, TN, preferred_element_type=F32)
        for cp in wide_copies(mb):
            cp.start()

        @pl.when(mb == 1)
        def _():
            scat_y.step(2)
            gather_dg.step(2)

        @pl.when(mb == 2)
        def _():
            scat_dh.step(2)
            gather_dg.step(3)
        return 0

    lax.fori_loop(0, n_m, wide_step, 0)
    for cp in wide_copies(n_m - 1):
        cp.wait()

    n_blk = wd_s.shape[1]

    def down_copies(nb):
        return [pltpu.make_async_copy(wd_s.at[pl.ds(e * ff, ff)], dwd_hbm.at[e, :, rows(nb * n_blk, n_blk)], out_sem.at[e]) for e in range(e_loc)]

    def down_step(nb, _):
        @pl.when(nb > 0)
        def _():
            for cp in down_copies(nb - 1):
                cp.wait()
        a = gated[...].reshape(n_tile * tile_rows, e_loc * ff)
        b = dys[:, :, rows(nb * n_blk, n_blk)].reshape(n_tile * tile_rows, n_blk)
        wd_s[...] = lax.dot_general(a, b, TN, preferred_element_type=F32)
        for cp in down_copies(nb):
            cp.start()
        return 0

    lax.fori_loop(0, d // n_blk, down_step, 0)
    for cp in down_copies(d // n_blk - 1):
        cp.wait()

    scat_y.step(3)
    gather_dg.step(4)
    gather_dg.step(5)
    gather_dg.step(6)
    d_router_t[...] = jnp.zeros_like(d_router_t)
    for t in range(n_tile):
        which, tl = t // side, t % side
        pieces = []
        for ep in range(side * CORES):
            px, pc = ep // CORES, ep % CORES
            total = None
            for py in range(side):
                if which == 0:
                    term = dgs[px, pl.ds((pc * side + py) * blk + tl * 8, 8)]
                else:
                    term = dgs[side + py, pl.ds((pc * side + px) * blk + tl * 8, 8)]
                total = term if total is None else total + term
            pieces.append(total)
        d_g = jnp.concatenate(pieces, axis=0)
        g_t = lax.dot_general(sel_t[...], hid[t, :, pl.ds(d, 128)], NT, preferred_element_type=F32)
        d_l = g_t * (d_g - jnp.sum(g_t * d_g, axis=0, keepdims=True))
        d_logits_t[t] = d_l
        d_router_t[...] += jnp.dot(d_l.astype(BF16), hid[t, :, pl.ds(0, d)], preferred_element_type=F32)

    scat_y.step(4)
    scat_dh.step(3)
    scat_y.step(5)
    scat_dh.step(4)
    scat_dh.step(5)
    for g in (gather_h, gather_dy, gather_dg):
        g.finish()
    for s in (scat_y, scat_dh):
        s.step(6)
        for t in range(n_tile):
            s.swap_copy(t, place, span).wait_send()


def moe(mesh, h_ext, dy, sel, sel_t, w_gate, w_up, w_down):
    side = mesh.shape["tp"]
    n_tok, d = dy.shape
    e_loc, _, ff = w_gate.shape
    tile_rows = CORES * side * n_tok // 2
    span = tile_rows // CORES
    n_tile = 2 * side
    n_ep = side * CORES
    dx = h_ext.shape[1]
    vm = pl.BlockSpec(memory_space=pltpu.VMEM)
    hbm = pl.BlockSpec(memory_space=pl.ANY)
    blk = n_tok // 2
    n_g, n_s = 2 * Gather.COPIES, 2 * Scatter.COPIES
    return pl.pallas_call(
        functools.partial(moe_kernel, side, d, e_loc, ff),
        out_shape=(
            jax.ShapeDtypeStruct((n_tok, d), F32),
            jax.ShapeDtypeStruct((n_tok, d), F32),
            jax.ShapeDtypeStruct((1, d), F32),
            jax.ShapeDtypeStruct((n_ep * 8, d), F32),
            jax.ShapeDtypeStruct((n_tile, n_ep * 8, tile_rows), F32),
            jax.ShapeDtypeStruct(w_gate.shape, F32),
            jax.ShapeDtypeStruct(w_up.shape, F32),
            jax.ShapeDtypeStruct(w_down.shape, F32),
        ),
        in_specs=[vm, vm, vm, vm, hbm, hbm, hbm],
        out_specs=(vm, vm, vm, vm, vm, hbm, hbm, hbm),
        scratch_shapes=[
            pltpu.VMEM((n_tile, tile_rows, dx), BF16),
            pltpu.VMEM((n_tile, tile_rows, d), BF16),
            pltpu.VMEM((n_tile, tile_rows, tile_rows), F32),
            pltpu.VMEM((n_tok, tile_rows), F32),
            pltpu.VMEM((d, 2 * e_loc * ff), BF16),
            pltpu.VMEM((e_loc * ff, d), BF16),
            pltpu.VMEM((n_tile, tile_rows, e_loc * ff), BF16),
            pltpu.VMEM((n_tile, tile_rows, 2 * e_loc * ff), BF16),
            pltpu.VMEM((n_tile, tile_rows, d), BF16),
            pltpu.VMEM((n_tile, tile_rows, d), BF16),
            pltpu.VMEM((2, n_tile, span, d), BF16),
            pltpu.VMEM((2, 3 * span, d), BF16),
            pltpu.VMEM((2, 3 * span, d), BF16),
            pltpu.VMEM((2, 3 * blk, d), BF16),
            pltpu.VMEM((2, 3 * blk, d), BF16),
            pltpu.VMEM((tile_rows, 2 * e_loc * ff), F32),
            pltpu.VMEM((tile_rows, e_loc * ff), F32),
            pltpu.VMEM((tile_rows, e_loc * ff), F32),
            pltpu.VMEM((e_loc * ff, 256), F32),
            pltpu.VMEM((n_tile, 1, d), F32),
            pltpu.SemaphoreType.DMA((3 * e_loc,)),
            pltpu.SemaphoreType.DMA((3, 2)),
            pltpu.SemaphoreType.DMA((3, n_g)),
            pltpu.SemaphoreType.DMA((3, n_g)),
            pltpu.SemaphoreType.DMA((2, n_s)),
            pltpu.SemaphoreType.DMA((2, n_s)),
            pltpu.SemaphoreType.DMA((2, n_tile)),
            pltpu.SemaphoreType.DMA((2, n_tile)),
            pltpu.SemaphoreType.DMA((2 * e_loc,)),
        ],
        compiler_params=pltpu.CompilerParams(collective_id=0, has_side_effects=True, vmem_limit_bytes=67043328),
        name="moe",
    )(h_ext, dy, sel, sel_t, w_gate, w_up, w_down)


def solution(mesh):
    tok_spec = P(("dp", "ep", "tp"), None)
    wide_spec = P("ep", None, "tp")
    down_spec = P("ep", "tp", None)
    grad_wide = P(("dp", "ep"), None, "tp")
    grad_down = P(("dp", "ep"), "tp", None)
    group = ("ep", "tp")
    side = mesh.shape["tp"]
    assert mesh.shape["ep"] == side * CORES

    def device_step(x_in, norm_gain, w_router, expert_idx, w_gate, w_up, w_down, out_bias, dy_out):
        n_tok, d_model = x_in.shape
        n_exp = w_router.shape[1]
        local_exp, _, ff = w_gate.shape
        n_ep = n_exp // local_exp
        blk = n_tok // 2
        x_f32 = x_in.astype(F32)
        inv_rms = lax.rsqrt(jnp.mean(x_f32 * x_f32, axis=-1, keepdims=True) + EPS)
        normed = x_f32 * inv_rms
        gain_f32 = norm_gain.astype(F32)
        hidden = (normed * gain_f32).astype(BF16)
        logits = jnp.dot(hidden, w_router, preferred_element_type=F32)
        chosen = expert_idx[:, :, None] == jnp.arange(n_exp)[None, None, :]
        mask = jnp.any(chosen, axis=1)
        top = jnp.max(jnp.where(mask, logits, -jnp.inf), axis=-1, keepdims=True)
        unnorm = jnp.where(mask, jnp.exp(jnp.minimum(logits - top, 0.0)), 0.0)
        gates = unnorm / jnp.sum(unnorm, axis=-1, keepdims=True)
        hi = lax.reduce_precision(gates, 8, 7)
        mid = lax.reduce_precision(gates - hi, 8, 7)
        lo = gates - hi - mid
        zeros = jnp.zeros((n_tok, 128 - 3 * n_exp), F32)
        h_ext = jnp.concatenate([hidden, jnp.concatenate([hi, mid, lo, zeros], axis=1).astype(BF16)], axis=1)
        ep, tp = lax.axis_index("ep"), lax.axis_index("tp")
        lane = jnp.arange(128)
        lane_e = jnp.where(lane < 3 * n_exp, lane % n_exp, n_exp)
        sel = (lane_e[:, None] == (ep * local_exp + jnp.arange(local_exp * ff) // ff)[None, :]).astype(BF16)
        slot = jnp.arange(n_ep * 8)
        slot_e = jnp.where(slot % 8 < local_exp, slot // 8 * local_exp + slot % 8, n_exp + 1)
        sel_t = (slot_e[:, None] == lane_e[None, :]).astype(BF16)
        y_sum, dh_sum, d_bias, dr_t, dl_t, d_gate, d_up, d_down = moe(mesh, h_ext, dy_out, sel, sel_t, w_gate, w_up, w_down)
        y_out = (x_f32 + y_sum + out_bias.astype(F32)).astype(BF16)
        d_router = dr_t.reshape(n_ep, 8, d_model)[:, :local_exp].reshape(n_exp, d_model).T
        x, c = ep // CORES, ep % CORES
        own_a = lax.dynamic_slice(dl_t, (x, 0, (c * side + tp) * blk), (1, n_ep * 8, blk))[0]
        own_b = lax.dynamic_slice(dl_t, (side + tp, 0, (c * side + x) * blk), (1, n_ep * 8, blk))[0]
        own_dl = jnp.concatenate([own_a, own_b], axis=1).reshape(n_ep, 8, n_tok)[:, :local_exp].reshape(n_exp, n_tok)
        dh_total = dh_sum + jnp.einsum("et,de->td", own_dl.astype(BF16), w_router, preferred_element_type=F32)
        d_gain = lax.psum(jnp.sum(dh_total * normed, axis=0), group)
        d_norm = dh_total * gain_f32
        dx_in = (dy_out.astype(F32) + inv_rms * (d_norm - normed * jnp.mean(d_norm * normed, axis=-1, keepdims=True))).astype(BF16)
        return y_out, dx_in, d_gain, d_router, d_gate, d_up, d_down, d_bias.reshape(d_model)

    return jax.shard_map(device_step, mesh=mesh, in_specs=(tok_spec, P(None), P(None, None), tok_spec, wide_spec, wide_spec, down_spec, P(None), tok_spec), out_specs=(tok_spec, tok_spec, P("dp"), P("dp", None), grad_wide, grad_wide, grad_down, P("dp")), check_vma=False)
```

time: 297 us -> 203 us (0.68)
  Pallas kernels: 0 us -> 127 us
  matrix products: 82.7 us -> 2.68 us
  blocking collectives: 118 us -> 48.6 us
  waiting for transfers between devices: 50.9 us -> 0 us
  between operations: 14 us -> 0.76 us
  local copies, waits for them, and re-layouts: 20 us -> 14.1 us
    pallas_call x0 -> x1, Pallas kernels: none -> 127 us  [moe(): pl.pallas_call(functools.partial(moe_kernel, side, d, e_loc, ff), out_sha...]
    dot_general x10 -> x2, matrix products: 66.7 us -> 2.68 us  [the longest x1 1.58 us: device_step(): jnp.einsum('et,de->td', own_dl.astype(BF16), w_router, preferred_element_...]
    all_gather x2 -> x0, blocking collectives: 54.5 us -> none  [the longest x1 34 us: device_step(): all_g = lax.all_gather(gates, group, axis=0, tiled=True)]
    all_gather x2 -> x0, waiting for transfers between devices: 33.4 us -> none  [the longest x1 28.9 us: device_step(): all_dy = lax.all_gather(dy_out, group, axis=0, tiled=True)]
    reduce_scatter x2 -> x0, waiting for transfers between devices: 16.6 us -> none  [the longest x1 16.6 us: device_step(): y_sum = lax.psum_scatter(part_out, group, scatter_dimension=0, tiled=True)]
    unnamed x2 -> x0, matrix products: 16 us -> none
    psum x1 -> x0, blocking collectives: 12.5 us -> none  [device_step(): lax.psum(d_gate_part, 'tp')]
    unnamed x36 -> x11, local copies, waits for them, and re-layouts: 19.8 us -> 10.5 us
  transfers between devices with their start and end apart: 4 -> 0, of which waited for: 3 -> 0; matrix products, arithmetic and copies ran while one was open for 28% -> 0% of each run, Pallas kernels for 0% -> 0%
where the time goes in v2:
time: 203 us
  Pallas kernels  127 us (63%)
  blocking collectives  48.6 us (24%)
  local copies, waits for them, and re-layouts  14.1 us (7%)
  other arithmetic  9.55 us (5%)
  matrix products  2.68 us (1%)
    pallas_call x1, Pallas kernels, moe(): pl.pallas_call(functools.partial(moe_kernel, side, d, e_loc, ff), out_sha...  127 us
    psum x1, blocking collectives, device_step(): d_gain = lax.psum(jnp.sum(dh_total * normed, axis=0), group)  48.6 us
    unnamed x11, local copies, waits for them, and re-layouts  10.5 us

profile of v2, /device:TPU:97, one launch (start us, length us, event | category | flops | bytes accessed | tf_op | source)
XLA Modules:
  0.0 202.9 jit_solution(11167806649040682093)
XLA Ops:
  0.6 1.1 fusion.11
  1.7 0.0 copy-start.3
  1.7 0.7 convert_element_type.33
  2.4 0.0 copy-start.2
  2.4 0.6 copy-done.2
  3.0 1.0 fusion.4
  4.1 0.0 copy-done.3
  4.1 0.7 fusion.14
  4.8 0.1 copy.24
  4.9 1.1 select_reduce_fusion
  6.0 0.1 copy.23
  6.1 0.2 fusion.17
  6.3 0.1 fusion.15
  6.4 0.8 concatenate.15.h_in
  7.2 0.8 compare_convert_fusion.sel
  8.0 0.7 compare_convert_fusion.1.sel_t
  8.7 127.2 %moe.1 = (f32[64,1536]{1,0:T(8,128)}, f32[64,1536]{1,0:T(8,128)}, f32[1,1536]{1,0:T(1,128)}, f32[64,1536]{1,0:T(8,128)}, f32[8,64,256]{2,1,0:T(8,128)}, /*index=...) custom-call(bf16[64,1664]{1,0:T(8,128)(2,1)} %concatenate.15.h_in, bf16[64,1536]{1,0:T(8,128)(2,1)} %dy_in.1, ...), custom_call_target="tpu_custom_call" | custom-call | tf_op jit(solution)/shard_map/moe/pallas_call | solution.py:415
  136.0 0.9 fusion.18
  136.8 0.1 pad_maximum_fusion
  136.9 1.6 fusion.10
  138.5 0.7 convert_element_type.37
  139.2 2.2 %fusion.9 = (bf16[64,1536]{1,0:T(8,128)(2,1)}, bf16[64,1536]{1,0:T(8,128)(2,1)}) fusion(bf16[64,1536]{1,0:T(8,128)(2,1)} %param.9, bf16[64,1536]{1,0:T(8,128)(2,1)} %dy_in.1, f32[64,1536]{1,0:T(8,128)S(1)} %get-tuple-element.36, f32[64]{0:T(128)S(1)} %broadcast_multiply_fusion, f32[1536]{0:T(1024)} %copy-done.2, f32[64]{0:T(128)} %copy-done.3, ...), kind=kLoop, calls=%fused_computation.13 | loop fusion | flops 1179648 | bytes 1585664 | tf_op jit(solution)/shard_map/convert_element_type | solution.py:514
  141.4 48.6 %psum.7 = f32[1536]{0:T(1024)} all-reduce(f32[1536]{0:T(1024)S(1)} %get-tuple-element.24), channel_id=1, replica_groups=mesh['dp'=1,'tp'=4,'ep'=8] {'ep','tp'}, use_global_device_ids=true, to_apply=%region_6.7 | all-reduce | flops 1536 | bytes 12288 | tf_op jit(solution)/shard_map/psum | solution.py:512
  189.9 1.7 reshape.114
  191.7 1.3 reduce
  193.0 0.0 copy-start.1
  193.0 4.4 %copy.28 = f32[5,1536,128]{2,1,0:T(8,128)} copy(f32[5,1536,128]{2,1,0:T(8,128)} %get-tuple-element.49) | data formatting | bytes 7864320
  197.4 0.0 copy-done.1
  197.4 0.0 copy-start
  197.4 2.0 copy.29
  199.4 1.5 copy-done
  201.0 1.9 copy.30
  (8 shorter events, 0.1 us)
Async XLA Ops:
  1.7 2.3 %copy-start.3 = (f32[64]{0:T(128)}, f32[64]{0:T(128)S(1)}, u32[]{:S(2)}) copy-start(f32[64]{0:T(128)S(1)} %add_rsqrt_fusion) | copy-start | bytes 772
  2.4 0.6 copy-start.2
  193.0 4.4 %copy-start.1 = (f32[5,1536,128]{2,1,0:T(8,128)S(1)}, f32[5,1536,128]{2,1,0:T(8,128)}, u32[]{:S(2)}) copy-start(f32[5,1536,128]{2,1,0:T(8,128)} %get-tuple-element.50) | copy-start | bytes 11796484
  197.4 3.5 %copy-start = (f32[5,128,1536]{2,1,0:T(8,128)S(1)}, f32[5,128,1536]{2,1,0:T(8,128)}, u32[]{:S(2)}) copy-start(f32[5,128,1536]{2,1,0:T(8,128)} %get-tuple-element.51) | copy-start | bytes 11796484

commit v3 on v2

v3 whole, which is shorter than its diff:
```python
import functools

import jax
import jax.numpy as jnp
from jax import lax
from jax.experimental import pallas as pl
from jax.experimental.pallas import tpu as pltpu
from jax.sharding import PartitionSpec as P

EPS = 1e-6
CORES = 2
BF16, F32 = jnp.bfloat16, jnp.float32
MESH = pl.DeviceIdType.MESH
NT = (((1,), (1,)), ((), ()))
TN = (((0,), (0,)), ((), ()))


def rows(start, size):
    return pl.ds(pl.multiple_of(start, size & -size), size)


class Place:
    def __init__(self, side):
        ep = lax.axis_index("ep")
        self.side = side
        self.x, self.c, self.y = lax.div(ep, CORES), lax.rem(ep, CORES), lax.axis_index("tp")

    def along(self, axis, step):
        if axis == "x":
            return {"ep": lax.rem(self.x + step + self.side, self.side) * CORES + self.c, "tp": self.y}
        return {"ep": self.x * CORES + self.c, "tp": lax.rem(self.y + step + self.side, self.side)}

    def partner(self):
        return {"ep": self.x * CORES + 1 - self.c, "tp": self.y}


class Half:
    def __init__(self, place, which, blk):
        self.p, self.which, self.blk, n = place, which, blk, place.side
        self.base = which * n
        self.major, self.minor = ("x", "y") if which == 0 else ("y", "x")
        self.m, self.n = (place.x, place.y) if which == 0 else (place.y, place.x)
        self.span = n * blk

    def tile(self, step):
        return self.base + lax.rem(self.m + step + self.p.side, self.p.side)

    def mine(self, part=0, parts=1):
        size = self.span // parts
        return rows(self.p.c * self.span + part * size, size)

    def block(self, step, part=0, parts=1):
        size = self.blk // parts
        return rows(self.p.c * self.span + lax.rem(self.n + step + self.p.side, self.p.side) * self.blk + part * size, size)


class Gather:
    COPIES = 17

    def __init__(self, halves, own, buf, send, recv):
        self.halves, self.own, self.buf, self.send, self.recv = halves, own, buf, send, recv

    def copy(self, h, k, src, dst, target):
        i = h.which * self.COPIES + k
        return pltpu.make_async_remote_copy(src_ref=src, dst_ref=dst, send_sem=self.send.at[i], recv_sem=self.recv.at[i], device_id=target, device_id_type=MESH)

    def make(self, h, k):
        b, p = self.buf, h.p
        same = lambda t, r, target: self.copy(h, k, b.at[t, r], b.at[t, r], target)
        s, d = 1 - 2 * (k % 2), k % 2
        if k < 2:
            return self.copy(h, k, self.own.at[pl.ds(h.which * h.blk, h.blk)], b.at[h.tile(0), h.block(0)], p.along(h.minor, s))
        if k < 4:
            return same(h.tile(0), h.block(-s, d, 2), p.along(h.minor, s))
        if k < 6:
            return same(h.tile(0), h.mine(d, 2), p.along(h.major, s))
        if k < 8:
            return same(h.tile(0), h.mine(1 - d, 2), p.along(h.major, s))
        if k < 10:
            return same(h.tile(-s), h.mine(d, 2), p.along(h.major, s))
        if k == 10:
            return same(h.tile(0), h.mine(), p.partner())
        step, part = ((-1, 0), (1, 1), (-1, 1), (1, 0), (2, 0), (2, 1))[k - 11]
        return same(h.tile(step), h.mine(part, 2), p.partner())

    def own_copy(self, h, sem):
        return pltpu.make_async_copy(self.own.at[pl.ds(h.which * h.blk, h.blk)], self.buf.at[h.tile(0), h.block(0)], sem)

    def start(self, *ks):
        for k in ks:
            for h in self.halves:
                self.make(h, k).start()

    def wait(self, *ks):
        for k in ks:
            for h in self.halves:
                self.make(h, k).wait_recv()

    def finish(self):
        for k in range(self.COPIES):
            for h in self.halves:
                self.make(h, k).wait_send()

    def begin(self, local):
        self.start(0, 1)
        for h in self.halves:
            self.own_copy(h, local.at[h.which]).start()

    def relay_minor(self, local):
        for h in self.halves:
            self.own_copy(h, local.at[h.which]).wait()
        self.wait(0, 1)
        self.start(2, 3)

    def share_own(self):
        self.wait(2, 3)
        self.start(10)

    def send_major(self):
        self.start(4, 5, 6, 7)

    def relay_major(self):
        self.wait(4, 5)
        self.start(8, 9, 11, 12)

    def share_near(self):
        self.wait(6, 7)
        self.start(13, 14)

    def share_far(self):
        self.wait(8, 9)
        self.start(15, 16)


class Scatter:
    COPIES = 12

    def __init__(self, halves, part, big, small, send, recv):
        self.halves, self.part, self.big, self.small, self.send, self.recv = halves, part, big, small, send, recv

    def piece(self, h, part, parts=2):
        size = h.span // parts
        return pl.ds(part * size, size)

    def block(self, h, step, part=0, parts=1):
        size = h.blk // parts
        return rows(lax.rem(h.n + step + h.p.side, h.p.side) * h.blk + part * size, size)

    def add(self, t, r, *terms):
        total = self.part[t, r].astype(F32)
        for term in terms:
            total = total + term.astype(F32)
        self.part[t, r] = total.astype(BF16)

    def land(self, h, k):
        if k < 6:
            return self.big.at[h.which, pl.ds(k * (h.span // 2), h.span // 2)]
        return self.small.at[h.which, pl.ds((k - 6) * (h.blk // 2), h.blk // 2)]

    def make(self, h, k):
        s, d = 1 - 2 * (k % 2), k % 2
        if k < 2:
            src = self.part.at[h.tile(2), self.piece(h, d)]
        elif k < 4:
            src = self.part.at[h.tile(s), self.piece(h, 1 - d)]
        elif k < 6:
            src = self.part.at[h.tile(s), self.piece(h, d)]
        elif k < 8:
            src = self.part.at[h.tile(0), self.block(h, 2, d, 2)]
        elif k < 10:
            src = self.part.at[h.tile(0), self.block(h, s, 1 - d, 2)]
        else:
            src = self.part.at[h.tile(0), self.block(h, s, d, 2)]
        i = h.which * self.COPIES + k
        axis = h.major if k < 6 else h.minor
        return pltpu.make_async_remote_copy(src_ref=src, dst_ref=self.land(h, k), send_sem=self.send.at[i], recv_sem=self.recv.at[i], device_id=h.p.along(axis, s), device_id_type=MESH)

    def start(self, h, *ks):
        for k in ks:
            self.make(h, k).start()

    def got(self, h, k):
        self.make(h, k).wait_recv()
        return self.land(h, k)[...]

    def begin(self):
        for h in self.halves:
            self.start(h, 0, 1)
        for h in self.halves:
            self.start(h, 2, 3)

    def relay_major(self):
        for h in self.halves:
            for d in (0, 1):
                self.add(h.tile(1 - 2 * d), self.piece(h, d), self.got(h, d))
                self.start(h, 4 + d)

    def turn(self):
        for h in self.halves:
            self.add(h.tile(0), self.piece(h, 0), self.got(h, 3), self.got(h, 4))
            self.add(h.tile(0), self.piece(h, 1), self.got(h, 2), self.got(h, 5))
            self.start(h, 6, 7, 8, 9)

    def relay_minor(self):
        for h in self.halves:
            for d in (0, 1):
                self.add(h.tile(0), self.block(h, 1 - 2 * d, d, 2), self.got(h, 6 + d))
                self.start(h, 10 + d)

    def total(self, h):
        mine = self.part[h.tile(0), self.block(h, 0)].astype(F32)
        low = self.got(h, 9).astype(F32) + self.got(h, 10).astype(F32)
        high = self.got(h, 8).astype(F32) + self.got(h, 11).astype(F32)
        return mine + jnp.concatenate([low, high], axis=0)

    def finish(self):
        for h in self.halves:
            for k in range(self.COPIES):
                self.make(h, k).wait_send()


def moe_kernel(side, d, e_loc, ff, n_exp, h_in, dy_in, x_ref, gain_ref, bias_ref, sel, sel_t, w_rt, pick, wg_hbm, wu_hbm, wd_hbm,
               y_ref, dx_ref, d_gain, d_bias, d_router_t, dwg_hbm, dwu_hbm, dwd_hbm,
               hid, dys, dgs, dg_own, w_gu, w_d, gated, d_gu, part_y, part_dh, stage, swap, big_y, big_dh, small_y, small_dh,
               gu, gx_s, da_s, wd_s, bias_s, dl_s, dr_s, ar1, ar2,
               w_sem, local, g_send, g_recv, s_send, s_recv, stage_send, swap_recv, credit, out_sem, ar_send, ar_recv):
    place = Place(side)
    n_tile = 2 * side
    n_ep = side * CORES
    blk = h_in.shape[0] // 2
    halves = [Half(place, 0, blk), Half(place, 1, blk)]
    tile_rows = hid.shape[1]
    span = tile_rows // CORES
    mine, theirs = rows(place.c * span, span), rows((1 - place.c) * span, span)
    me_ep = lax.axis_index("ep")

    weights = []
    for e in range(e_loc):
        weights.append(pltpu.make_async_copy(wg_hbm.at[e], w_gu.at[:, pl.ds(2 * e * ff, ff)], w_sem.at[3 * e]))
        weights.append(pltpu.make_async_copy(wu_hbm.at[e], w_gu.at[:, pl.ds((2 * e + 1) * ff, ff)], w_sem.at[3 * e + 1]))
        weights.append(pltpu.make_async_copy(wd_hbm.at[e], w_d.at[pl.ds(e * ff, ff)], w_sem.at[3 * e + 2]))

    ep_peers = [{"ep": lax.rem(me_ep + o, n_ep), "tp": place.y} for o in range(1, n_ep)]
    tp_peers = [{"ep": me_ep, "tp": lax.rem(place.y + o, side)} for o in range(1, side)]
    barrier = pltpu.get_barrier_semaphore()
    for peer in ep_peers + tp_peers:
        pl.semaphore_signal(barrier, inc=1, device_id=peer, device_id_type=MESH)
    for w in weights:
        w.start()
    pl.semaphore_wait(barrier, n_ep + side - 2)

    gather_h = Gather(halves, h_in, hid, g_send.at[0], g_recv.at[0])
    gather_dy = Gather(halves, dy_in, dys, g_send.at[1], g_recv.at[1])
    gather_dg = Gather(halves, dg_own, dgs, g_send.at[2], g_recv.at[2])
    scat_y = Scatter(halves, part_y, big_y, small_y, s_send.at[0], s_recv.at[0])
    scat_dh = Scatter(halves, part_dh, big_dh, small_dh, s_send.at[1], s_recv.at[1])

    gather_h.begin(local.at[0])
    gather_dy.begin(local.at[1])
    gather_h.relay_minor(local.at[0])
    gather_dy.relay_minor(local.at[1])
    gather_h.share_own()
    gather_h.send_major()
    gather_dy.share_own()
    for w in weights:
        w.wait()

    lane = lax.broadcasted_iota(jnp.int32, (tile_rows, 128), 1)

    def index_of(s):
        i = s - 2 * jnp.minimum(1, lax.div(s, 2)) - 6 * jnp.minimum(1, lax.div(s, 10))
        j, which = lax.div(i, 2), lax.rem(i, 2)
        off = j + lax.div(j, 2) - 2 * lax.div(j, 3)
        return which * side + lax.rem(place.x * (1 - which) + place.y * which + off, side)

    def is_back(s):
        return jnp.logical_or(jnp.logical_and(s >= 2, s < 4), s >= 10)

    def swap_copy(s, kind, t):
        slot = lax.rem(s, 2)
        return pltpu.make_async_remote_copy(src_ref=stage.at[slot, theirs], dst_ref=swap.at[t], send_sem=stage_send.at[slot], recv_sem=swap_recv.at[kind, t], device_id=place.partner(), device_id_type=MESH)

    def settle(s):
        t = index_of(s)

        def take(kind, part):
            swap_copy(s, kind, t).wait_recv()
            part[t] = (part[t].astype(F32) + swap[t].astype(F32)).astype(BF16)

        @pl.when(jnp.logical_not(is_back(s)))
        def _():
            take(0, part_y)
            pl.semaphore_signal(credit, inc=1, device_id=place.partner(), device_id_type=MESH)

        @pl.when(is_back(s))
        def _():
            take(1, part_dh)

    def hand_over(s, kind, t, part, value):
        @pl.when(s >= 1)
        def _():
            settle(s - 1)

        @pl.when(s >= 2)
        def _():
            swap_copy(s, kind, t).wait_send()

        slot = lax.rem(s, 2)
        stage[slot] = value().astype(BF16)
        part[t] = stage[slot, mine]
        if kind == 1:
            pl.semaphore_wait(credit, 1)
        swap_copy(s, kind, t).start()

    def tile_step(s, _):
        t = index_of(s)

        def at(k, *actions):
            @pl.when(s == k)
            def _():
                for action in actions:
                    action()

        at(0, lambda: gather_h.wait(10))
        at(2, gather_h.relay_major, gather_dy.send_major, lambda: gather_dy.wait(10))
        at(4, gather_h.share_near, lambda: gather_h.wait(11, 12, 13, 14))
        at(6, gather_h.share_far)
        at(7, gather_dy.relay_major)
        at(8, lambda: gather_h.wait(15, 16))
        at(10, gather_dy.share_near, lambda: gather_dy.wait(11, 12, 13, 14))
        at(11, scat_y.begin)
        at(12, gather_dy.share_far)
        at(14, lambda: gather_dy.wait(15, 16), scat_y.relay_major)

        @pl.when(jnp.logical_not(is_back(s)))
        def _():
            gu[t] = jnp.dot(hid[t, :, pl.ds(0, d)], w_gu[...], preferred_element_type=F32)
            gx_s[...] = jnp.dot(hid[t, :, pl.ds(d, 128)], sel[...], preferred_element_type=F32)
            for e in range(e_loc):
                pre, up = gu[t, :, pl.ds(2 * e * ff, ff)], gu[t, :, pl.ds((2 * e + 1) * ff, ff)]
                act = pre * jax.nn.sigmoid(pre) * up
                gated[t, :, pl.ds(e * ff, ff)] = (act * gx_s[:, pl.ds(e * ff, ff)]).astype(BF16)
            hand_over(s, 0, t, part_y, lambda: jnp.dot(gated[t], w_d[...], preferred_element_type=F32))

        @pl.when(is_back(s))
        def _():
            gx_s[...] = jnp.dot(hid[t, :, pl.ds(d, 128)], sel[...], preferred_element_type=F32)
            da_s[...] = lax.dot_general(dys[t], w_d[...], NT, preferred_element_type=F32)
            bias_s[t] = jnp.sum(dys[t].astype(F32), axis=0, keepdims=True)
            sums = jnp.zeros((tile_rows, 128), F32)
            for e in range(e_loc):
                pre, up = gu[t, :, pl.ds(2 * e * ff, ff)], gu[t, :, pl.ds((2 * e + 1) * ff, ff)]
                gate, da = gx_s[:, pl.ds(e * ff, ff)], da_s[:, pl.ds(e * ff, ff)]
                sigma = jax.nn.sigmoid(pre)
                silu = pre * sigma
                sums = sums + jnp.where(lane == e, jnp.sum(silu * up * da, axis=1, keepdims=True), 0.0)
                da = da * gate
                d_gu[t, :, pl.ds(2 * e * ff, ff)] = (da * up * sigma * (1.0 + pre * (1.0 - sigma))).astype(BF16)
                d_gu[t, :, pl.ds((2 * e + 1) * ff, ff)] = (da * silu).astype(BF16)
            dg_own[rows(t * 8, 8)] = jnp.transpose(sums)[:8]
            hand_over(s, 1, t, part_dh, lambda: lax.dot_general(d_gu[t], w_gu[...], NT, preferred_element_type=F32))

        return 0

    steps = 2 * n_tile
    lax.fori_loop(0, steps, tile_step, 0)

    gather_dg.begin(local.at[2])
    settle(steps - 1)
    scat_dh.begin()
    d_bias[...] = jnp.sum(bias_s[...], axis=0)

    m_blk = tile_rows
    n_m = d // m_blk

    def wide_copies(mb):
        out = []
        for e in range(e_loc):
            for j, ref in enumerate((dwg_hbm, dwu_hbm)):
                out.append(pltpu.make_async_copy(gu.at[mb, :, pl.ds((2 * e + j) * ff, ff)], ref.at[e, rows(mb * m_blk, m_blk)], out_sem.at[mb, 2 * e + j]))
        return out

    def wide_step(mb, _):
        a = hid[:, :, rows(mb * m_blk, m_blk)].reshape(n_tile * tile_rows, m_blk)
        b = d_gu[...].reshape(n_tile * tile_rows, 2 * e_loc * ff)
        gu[mb] = lax.dot_general(a, b, TN, preferred_element_type=F32)
        for cp in wide_copies(mb):
            cp.start()

        def after(k, *actions):
            @pl.when(mb == k)
            def _():
                for action in actions:
                    action()

        after(0, lambda: gather_dg.relay_minor(local.at[2]), scat_y.turn)
        after(1, gather_dg.share_own, gather_dg.send_major)
        after(2, scat_y.relay_minor, scat_dh.relay_major)
        after(4, gather_dg.relay_major)
        after(5, gather_dg.share_near)
        return 0

    lax.fori_loop(0, n_m, wide_step, 0)

    for h in halves:
        r = pl.ds(h.which * blk, blk)
        y_ref[r] = (x_ref[r].astype(F32) + scat_y.total(h) + bias_ref[...].astype(F32)).astype(BF16)

    n_blk = wd_s.shape[2]
    n_n = d // n_blk

    def down_copies(nb):
        slot = lax.rem(nb, 2)
        return [pltpu.make_async_copy(wd_s.at[slot, pl.ds(e * ff, ff)], dwd_hbm.at[e, :, rows(nb * n_blk, n_blk)], out_sem.at[n_m + slot, e]) for e in range(e_loc)]

    def down_step(nb, _):
        @pl.when(nb > 1)
        def _():
            for cp in down_copies(nb - 2):
                cp.wait()
        a = gated[...].reshape(n_tile * tile_rows, e_loc * ff)
        b = dys[:, :, rows(nb * n_blk, n_blk)].reshape(n_tile * tile_rows, n_blk)
        wd_s[lax.rem(nb, 2)] = lax.dot_general(a, b, TN, preferred_element_type=F32)
        for cp in down_copies(nb):
            cp.start()

        @pl.when(nb == 0)
        def _():
            gather_dg.share_far()

        @pl.when(nb == 2)
        def _():
            scat_dh.turn()

        @pl.when(nb == 4)
        def _():
            scat_dh.relay_minor()
        return 0

    lax.fori_loop(0, n_n, down_step, 0)

    gather_dg.wait(10, 11, 12, 13, 14, 15, 16)
    dr_s[...] = jnp.zeros_like(dr_s)
    for t in range(n_tile):
        which, tl = t // side, t % side
        pieces = []
        for ep in range(n_ep):
            px, pc = ep // CORES, ep % CORES
            total = None
            for py in range(side):
                if which == 0:
                    term = dgs[px, pl.ds((pc * side + py) * blk + tl * 8, 8)]
                else:
                    term = dgs[side + py, pl.ds((pc * side + px) * blk + tl * 8, 8)]
                total = term if total is None else total + term
            pieces.append(total)
        d_g = jnp.concatenate(pieces, axis=0)
        g_t = lax.dot_general(sel_t[...], hid[t, :, pl.ds(d, 128)], NT, preferred_element_type=F32)
        d_l = (g_t * (d_g - jnp.sum(g_t * d_g, axis=0, keepdims=True))).astype(BF16)
        dl_s[t] = d_l
        dr_s[...] += jnp.dot(d_l, hid[t, :, pl.ds(0, d)], preferred_element_type=F32)
    d_router_t[...] = jnp.dot(pick[...], dr_s[...], preferred_element_type=F32, precision=lax.Precision.HIGHEST)

    gain = gain_ref[...].astype(F32)
    gain_part = jnp.zeros((1, d), F32)
    for h in halves:
        r = pl.ds(h.which * blk, blk)
        routed = lax.dot_general(dl_s[h.tile(0), :, mine], w_rt[...], TN, preferred_element_type=F32)
        own = jnp.zeros((blk, d), F32)
        for q in range(side):
            own = own + jnp.where(h.n == q, routed[q * blk:(q + 1) * blk], 0.0)
        x_f32 = x_ref[r].astype(F32)
        inv_rms = lax.rsqrt(jnp.mean(x_f32 * x_f32, axis=1, keepdims=True) + EPS)
        normed = x_f32 * inv_rms
        dh = scat_dh.total(h) + own
        gain_part = gain_part + jnp.sum(dh * normed, axis=0, keepdims=True)
        d_norm = dh * gain
        dx_ref[r] = (dy_in[r].astype(F32) + inv_rms * (d_norm - normed * jnp.mean(d_norm * normed, axis=1, keepdims=True))).astype(BF16)

    def spread(buf, slot, peers, first):
        out = []
        for o, peer in enumerate(peers):
            out.append(pltpu.make_async_remote_copy(src_ref=buf.at[slot], dst_ref=buf.at[slot], send_sem=ar_send.at[first + o], recv_sem=ar_recv.at[first + o], device_id=peer, device_id_type=MESH))
        for cp in out:
            cp.start()
        for cp in out:
            cp.wait_recv()
        return out

    ar1[me_ep] = gain_part
    sent = spread(ar1, me_ep, ep_peers, 0)
    ar2[place.y] = jnp.sum(ar1[...], axis=0)
    sent += spread(ar2, place.y, tp_peers, n_ep - 1)
    d_gain[...] = jnp.sum(ar2[...], axis=0)

    for cp in sent:
        cp.wait_send()
    for g in (gather_h, gather_dy, gather_dg):
        g.finish()
    for sc in (scat_y, scat_dh):
        sc.finish()
    for s in (steps - 2, steps - 1):
        swap_copy(s, 1, index_of(s)).wait_send()
    for mb in range(n_m):
        for cp in wide_copies(mb):
            cp.wait()
    for nb in (n_n - 2, n_n - 1):
        for cp in down_copies(nb):
            cp.wait()


def moe(mesh, h_ext, dy, x_in, gain, bias, sel, sel_t, w_rt, pick, w_gate, w_up, w_down):
    side = mesh.shape["tp"]
    n_tok, d = dy.shape
    e_loc, _, ff = w_gate.shape
    tile_rows = CORES * side * n_tok // 2
    span = tile_rows // CORES
    n_tile = 2 * side
    n_ep = side * CORES
    n_exp = n_ep * e_loc
    dx = h_ext.shape[1]
    vm = pl.BlockSpec(memory_space=pltpu.VMEM)
    hbm = pl.BlockSpec(memory_space=pl.ANY)
    blk = n_tok // 2
    n_g, n_s = 2 * Gather.COPIES, 2 * Scatter.COPIES
    n_peer = n_ep + side - 2
    return pl.pallas_call(
        functools.partial(moe_kernel, side, d, e_loc, ff, n_exp),
        out_shape=(
            jax.ShapeDtypeStruct((n_tok, d), BF16),
            jax.ShapeDtypeStruct((n_tok, d), BF16),
            jax.ShapeDtypeStruct((1, d), F32),
            jax.ShapeDtypeStruct((1, d), F32),
            jax.ShapeDtypeStruct((n_exp, d), F32),
            jax.ShapeDtypeStruct(w_gate.shape, F32),
            jax.ShapeDtypeStruct(w_up.shape, F32),
            jax.ShapeDtypeStruct(w_down.shape, F32),
        ),
        in_specs=[vm] * 9 + [hbm] * 3,
        out_specs=(vm, vm, vm, vm, vm, hbm, hbm, hbm),
        scratch_shapes=[
            pltpu.VMEM((n_tile, tile_rows, dx), BF16),
            pltpu.VMEM((n_tile, tile_rows, d), BF16),
            pltpu.VMEM((n_tile, tile_rows, tile_rows), F32),
            pltpu.VMEM((n_tok, tile_rows), F32),
            pltpu.VMEM((d, 2 * e_loc * ff), BF16),
            pltpu.VMEM((e_loc * ff, d), BF16),
            pltpu.VMEM((n_tile, tile_rows, e_loc * ff), BF16),
            pltpu.VMEM((n_tile, tile_rows, 2 * e_loc * ff), BF16),
            pltpu.VMEM((n_tile, span, d), BF16),
            pltpu.VMEM((n_tile, span, d), BF16),
            pltpu.VMEM((2, tile_rows, d), BF16),
            pltpu.VMEM((n_tile, span, d), BF16),
            pltpu.VMEM((2, 3 * span, d), BF16),
            pltpu.VMEM((2, 3 * span, d), BF16),
            pltpu.VMEM((2, 3 * blk, d), BF16),
            pltpu.VMEM((2, 3 * blk, d), BF16),
            pltpu.VMEM((n_tile, tile_rows, 2 * e_loc * ff), F32),
            pltpu.VMEM((tile_rows, e_loc * ff), F32),
            pltpu.VMEM((tile_rows, e_loc * ff), F32),
            pltpu.VMEM((2, e_loc * ff, 256), F32),
            pltpu.VMEM((n_tile, 1, d), F32),
            pltpu.VMEM((n_tile, n_ep * 8, tile_rows), BF16),
            pltpu.VMEM((n_ep * 8, d), F32),
            pltpu.VMEM((n_ep, 1, d), F32),
            pltpu.VMEM((side, 1, d), F32),
            pltpu.SemaphoreType.DMA((3 * e_loc,)),
            pltpu.SemaphoreType.DMA((3, 2)),
            pltpu.SemaphoreType.DMA((3, n_g)),
            pltpu.SemaphoreType.DMA((3, n_g)),
            pltpu.SemaphoreType.DMA((2, n_s)),
            pltpu.SemaphoreType.DMA((2, n_s)),
            pltpu.SemaphoreType.DMA((2,)),
            pltpu.SemaphoreType.DMA((2, n_tile)),
            pltpu.SemaphoreType.REGULAR,
            pltpu.SemaphoreType.DMA((d // tile_rows + 2, 2 * e_loc)),
            pltpu.SemaphoreType.DMA((n_peer,)),
            pltpu.SemaphoreType.DMA((n_peer,)),
        ],
        compiler_params=pltpu.CompilerParams(collective_id=0, has_side_effects=True, vmem_limit_bytes=67043328),
        name="moe",
    )(h_ext, dy, x_in, gain, bias, sel, sel_t, w_rt, pick, w_gate, w_up, w_down)


def solution(mesh):
    tok_spec = P(("dp", "ep", "tp"), None)
    wide_spec = P("ep", None, "tp")
    down_spec = P("ep", "tp", None)
    grad_wide = P(("dp", "ep"), None, "tp")
    grad_down = P(("dp", "ep"), "tp", None)
    side = mesh.shape["tp"]
    assert mesh.shape["ep"] == side * CORES

    def device_step(x_in, norm_gain, w_router, expert_idx, w_gate, w_up, w_down, out_bias, dy_out):
        n_tok, d_model = x_in.shape
        n_exp = w_router.shape[1]
        local_exp, _, ff = w_gate.shape
        n_ep = n_exp // local_exp
        x_f32 = x_in.astype(F32)
        inv_rms = lax.rsqrt(jnp.mean(x_f32 * x_f32, axis=-1, keepdims=True) + EPS)
        hidden = (x_f32 * inv_rms * norm_gain.astype(F32)).astype(BF16)
        logits = jnp.dot(hidden, w_router, preferred_element_type=F32)
        chosen = expert_idx[:, :, None] == jnp.arange(n_exp)[None, None, :]
        mask = jnp.any(chosen, axis=1)
        top = jnp.max(jnp.where(mask, logits, -jnp.inf), axis=-1, keepdims=True)
        unnorm = jnp.where(mask, jnp.exp(jnp.minimum(logits - top, 0.0)), 0.0)
        gates = unnorm / jnp.sum(unnorm, axis=-1, keepdims=True)
        hi = lax.reduce_precision(gates, 8, 7)
        mid = lax.reduce_precision(gates - hi, 8, 7)
        lo = gates - hi - mid
        zeros = jnp.zeros((n_tok, 128 - 3 * n_exp), F32)
        h_ext = jnp.concatenate([hidden, jnp.concatenate([hi, mid, lo, zeros], axis=1).astype(BF16)], axis=1)
        ep = lax.axis_index("ep")
        lane = jnp.arange(128)
        lane_e = jnp.where(lane < 3 * n_exp, lane % n_exp, n_exp)
        sel = (lane_e[:, None] == (ep * local_exp + jnp.arange(local_exp * ff) // ff)[None, :]).astype(BF16)
        slot = jnp.arange(n_ep * 8)
        slot_e = jnp.where(slot % 8 < local_exp, slot // 8 * local_exp + slot % 8, n_exp + 1)
        sel_t = (slot_e[:, None] == lane_e[None, :]).astype(BF16)
        pick = (jnp.arange(n_exp)[:, None] == slot_e[None, :]).astype(F32)
        w_rt = jnp.pad(w_router.T.reshape(n_ep, local_exp, d_model), ((0, 0), (0, 8 - local_exp), (0, 0))).reshape(n_ep * 8, d_model)
        row = lambda v: v.reshape(1, d_model)
        y_out, dx_in, d_gain, d_bias, d_router_t, d_gate, d_up, d_down = moe(mesh, h_ext, dy_out, x_in, row(norm_gain), row(out_bias), sel, sel_t, w_rt, pick, w_gate, w_up, w_down)
        return y_out, dx_in, d_gain.reshape(d_model), d_router_t.T, d_gate, d_up, d_down, d_bias.reshape(d_model)

    return jax.shard_map(device_step, mesh=mesh, in_specs=(tok_spec, P(None), P(None, None), tok_spec, wide_spec, wide_spec, down_spec, P(None), tok_spec), out_specs=(tok_spec, tok_spec, P("dp"), P("dp", None), grad_wide, grad_wide, grad_down, P("dp")), check_vma=False)
```

time: 203 us -> 151 us (0.74)
  blocking collectives: 48.6 us -> 0 us
  Pallas kernels: 127 us -> 120 us
  local copies, waits for them, and re-layouts: 14.1 us -> 20 us
    psum x1 -> x0, blocking collectives: 48.6 us -> none  [device_step(): d_gain = lax.psum(jnp.sum(dh_total * normed, axis=0), group)]
    pallas_call x1, Pallas kernels: 127 us -> 120 us  [moe(): pl.pallas_call(functools.partial(moe_kernel, side, d, e_loc, ff, n_exp),...]
    unnamed x11 -> x10, local copies, waits for them, and re-layouts: 10.5 us -> 14.8 us
    reshape x1 -> x4, local copies, waits for them, and re-layouts: 1.73 us -> 4.24 us  [the longest x2 2.57 us: device_step(): row = lambda v: v.reshape(1, d_model)]
    convert_element_type x4 -> x3, other arithmetic: 4.58 us -> 2.35 us  [the longest x2 1.74 us: device_step(): hidden = (x_f32 * inv_rms * norm_gain.astype(F32)).astype(BF16)]
where the time goes in v3:
time: 151 us; the launch traced here: 150 us
  Pallas kernels  120 us (79%)
  local copies, waits for them, and re-layouts  20 us (13%)
  other arithmetic  8.53 us (6%)
    pallas_call x1, Pallas kernels, moe(): pl.pallas_call(functools.partial(moe_kernel, side, d, e_loc, ff, n_exp),...  120 us
    unnamed x10, local copies, waits for them, and re-layouts  14.8 us

profile of v3, /device:TPU:97, one launch (start us, length us, event | category | flops | bytes accessed | tf_op | source)
XLA Modules:
  0.0 150.1 jit_solution(2718129140928752768)
XLA Ops:
  0.6 0.7 convert_element_type.22
  1.3 1.1 fusion
  2.4 1.1 fusion.2
  3.5 0.7 fusion.3
  4.2 1.1 select_reduce_fusion
  5.3 0.1 copy.23
  5.4 0.1 copy.24
  5.5 0.2 fusion.6
  5.7 0.1 fusion.4
  5.8 0.8 concatenate.6.h_in
  6.6 0.7 compare_convert_fusion.1.sel_t
  7.3 0.8 compare_convert_fusion.sel
  8.1 0.6 fusion.7.pick
  8.7 1.0 reshape.134
  9.6 0.7 pad_bitcast_fusion.w_rt
  10.3 1.3 reshape.132.gain_ref
  11.6 1.3 reshape.133.bias_ref
  12.9 119.8 %moe.1 = (bf16[64,1536]{1,0:T(8,128)(2,1)}, bf16[64,1536]{1,0:T(8,128)(2,1)}, f32[1,1536]{1,0:T(1,128)}, f32[1,1536]{1,0:T(1,128)}, f32[40,1536]{1,0:T(8,128)}, ...) custom-call(bf16[64,1664]{1,0:T(8,128)(2,1)} %concatenate.6.h_in, ...), custom_call_target="tpu_custom_call" | custom-call | tf_op jit(solution)/shard_map/moe/pallas_call | solution.py:527
  132.7 1.3 reduce
  134.0 1.3 reduce.1
  135.3 1.6 %copy.31 = bf16[64,1536]{1,0:T(8,128)(2,1)} copy(bf16[64,1536]{1,0:T(8,128)(2,1)} %get-tuple-element.38) | data formatting | bytes 393216
  136.9 1.6 %copy.32 = bf16[64,1536]{1,0:T(8,128)(2,1)} copy(bf16[64,1536]{1,0:T(8,128)(2,1)} %get-tuple-element.39) | data formatting | bytes 393216
  138.5 1.7 %copy.33 = f32[1536,40]{0,1:T(8,128)} copy(f32[1536,40]{0,1:T(8,128)} %bitcast.7) | data formatting | bytes 491520
  140.2 0.0 copy-start.1
  140.2 4.4 %copy.34 = f32[5,1536,128]{2,1,0:T(8,128)} copy(f32[5,1536,128]{2,1,0:T(8,128)} %get-tuple-element.42) | data formatting | bytes 7864320
  144.6 0.0 copy-done.1
  144.6 0.0 copy-start
  144.6 2.0 %copy.35 = f32[5,1536,128]{2,1,0:T(8,128)} copy(f32[5,1536,128]{2,1,0:T(8,128)S(1)} %copy-done.1) | data formatting | bytes 7864320
  146.6 1.5 %copy-done = f32[5,128,1536]{2,1,0:T(8,128)S(1)} copy-done((f32[5,128,1536]{2,1,0:T(8,128)S(1)}, f32[5,128,1536]{2,1,0:T(8,128)}, u32[]{:S(2)}) %copy-start) | copy-done | bytes 3932184
  148.2 1.9 %copy.36 = f32[5,128,1536]{2,1,0:T(8,128)} copy(f32[5,128,1536]{2,1,0:T(8,128)S(1)} %copy-done) | data formatting | bytes 7864320
  (6 shorter events, 0.0 us)
Async XLA Ops:
  140.2 4.4 %copy-start.1 = (f32[5,1536,128]{2,1,0:T(8,128)S(1)}, f32[5,1536,128]{2,1,0:T(8,128)}, u32[]{:S(2)}) copy-start(f32[5,1536,128]{2,1,0:T(8,128)} %get-tuple-element.43) | copy-start | bytes 11796484
  144.6 3.5 %copy-start = (f32[5,128,1536]{2,1,0:T(8,128)S(1)}, f32[5,128,1536]{2,1,0:T(8,128)}, u32[]{:S(2)}) copy-start(f32[5,128,1536]{2,1,0:T(8,128)} %get-tuple-element.44) | copy-start | bytes 11796484

commit v4 on v3

--- a/solution.py
+++ b/solution.py
@@ -183,11 +183,17 @@
         self.make(h, k).wait_recv()
         return self.land(h, k)[...]
 
+    def begin_far(self):
+        for h in self.halves:
+            self.start(h, 0, 1)
+
+    def begin_near(self):
+        for h in self.halves:
+            self.start(h, 2, 3)
+
     def begin(self):
-        for h in self.halves:
-            self.start(h, 0, 1)
-        for h in self.halves:
-            self.start(h, 2, 3)
+        self.begin_far()
+        self.begin_near()
 
     def relay_major(self):
         for h in self.halves:
@@ -219,15 +225,16 @@
                 self.make(h, k).wait_send()
 
 
-def moe_kernel(side, d, e_loc, ff, n_exp, h_in, dy_in, x_ref, gain_ref, bias_ref, sel, sel_t, w_rt, pick, wg_hbm, wu_hbm, wd_hbm,
+def moe_kernel(side, d, e_loc, ff, n_exp, dy_in, x_ref, gain_ref, bias_ref, w_r, idx_ref, wg_hbm, wu_hbm, wd_hbm,
                y_ref, dx_ref, d_gain, d_bias, d_router_t, dwg_hbm, dwu_hbm, dwd_hbm,
                hid, dys, dgs, dg_own, w_gu, w_d, gated, d_gu, part_y, part_dh, stage, swap, big_y, big_dh, small_y, small_dh,
-               gu, gx_s, da_s, wd_s, bias_s, dl_s, dr_s, ar1, ar2,
+               gu, gx_s, da_s, wd_s, bias_s, dl_s, dr_s, ar1, ar2, h_in, sel, sel_t, w_rt,
                w_sem, local, g_send, g_recv, s_send, s_recv, stage_send, swap_recv, credit, out_sem, ar_send, ar_recv):
     place = Place(side)
     n_tile = 2 * side
     n_ep = side * CORES
-    blk = h_in.shape[0] // 2
+    n_tok = x_ref.shape[0]
+    blk = n_tok // 2
     halves = [Half(place, 0, blk), Half(place, 1, blk)]
     tile_rows = hid.shape[1]
     span = tile_rows // CORES
@@ -247,6 +254,40 @@
         pl.semaphore_signal(barrier, inc=1, device_id=peer, device_id_type=MESH)
     for w in weights:
         w.start()
+
+    def lane_expert(shape, axis):
+        at = lax.broadcasted_iota(jnp.int32, shape, axis)
+        at = jnp.where(at >= 2 * n_exp, at - 2 * n_exp, jnp.where(at >= n_exp, at - n_exp, at))
+        return jnp.where(at < n_exp, at, n_exp)
+
+    def slot_expert(shape, axis):
+        at = lax.broadcasted_iota(jnp.int32, shape, axis)
+        low = jnp.bitwise_and(at, 7)
+        return jnp.where(low < e_loc, jnp.right_shift(at, 3) * e_loc + low, n_exp + 1)
+
+    def one_hot(cond, dtype=BF16):
+        return jnp.where(cond, 1.0, 0.0).astype(dtype)
+
+    def expert_row(shape):
+        return lax.broadcasted_iota(jnp.int32, shape, 0)
+
+    row_f32 = lambda ref: ref[...].astype(F32).reshape(1, d)
+    x_f32 = x_ref[...].astype(F32)
+    hidden = (x_f32 * lax.rsqrt(jnp.mean(x_f32 * x_f32, axis=1, keepdims=True) + EPS) * row_f32(gain_ref)).astype(BF16)
+    h_in[:, pl.ds(0, d)] = hidden
+    w_rep = lax.dot_general(one_hot(expert_row((n_exp, 128)) == lane_expert((n_exp, 128), 1)), w_r[...], TN, preferred_element_type=F32)
+    logits = lax.dot_general(hidden, w_rep.astype(BF16), NT, preferred_element_type=F32)
+    tok_expert = lane_expert((n_tok, 128), 1)
+    chosen = idx_ref[:, 0:1] == tok_expert
+    for j in range(1, idx_ref.shape[1]):
+        chosen = jnp.logical_or(chosen, idx_ref[:, j:j + 1] == tok_expert)
+    top = jnp.max(jnp.where(chosen, logits, -jnp.inf), axis=1, keepdims=True)
+    unnorm = jnp.where(chosen, jnp.exp(jnp.minimum(logits - top, 0.0)), 0.0)
+    tok_lane = lax.broadcasted_iota(jnp.int32, (n_tok, 128), 1)
+    gates = unnorm / jnp.sum(jnp.where(tok_lane < n_exp, unnorm, 0.0), axis=1, keepdims=True)
+    hi = gates.astype(BF16).astype(F32)
+    mid = (gates - hi).astype(BF16).astype(F32)
+    h_in[:, pl.ds(d, 128)] = jnp.where(tok_lane < n_exp, hi, jnp.where(tok_lane < 2 * n_exp, mid, gates - hi - mid)).astype(BF16)
     pl.semaphore_wait(barrier, n_ep + side - 2)
 
     gather_h = Gather(halves, h_in, hid, g_send.at[0], g_recv.at[0])
@@ -257,24 +298,29 @@
 
     gather_h.begin(local.at[0])
     gather_dy.begin(local.at[1])
+    for e in range(e_loc):
+        sel[:, pl.ds(e * ff, ff)] = one_hot(lane_expert((128, ff), 0) == me_ep * e_loc + e)
+    sel_t[...] = one_hot(slot_expert(sel_t.shape, 0) == lane_expert(sel_t.shape, 1))
+    pick = slot_expert((n_exp, 8 * n_ep), 1) == expert_row((n_exp, 8 * n_ep))
+    w_rt[...] = lax.dot_general(one_hot(pick), w_r[...], TN, preferred_element_type=F32).astype(BF16)
     gather_h.relay_minor(local.at[0])
     gather_dy.relay_minor(local.at[1])
     gather_h.share_own()
     gather_h.send_major()
-    gather_dy.share_own()
     for w in weights:
         w.wait()
 
     lane = lax.broadcasted_iota(jnp.int32, (tile_rows, 128), 1)
 
     def index_of(s):
-        i = s - 2 * jnp.minimum(1, lax.div(s, 2)) - 6 * jnp.minimum(1, lax.div(s, 10))
+        back = lax.div(s, n_tile)
+        i = s * (1 - back) + (2 * n_tile - 1 - s) * back
         j, which = lax.div(i, 2), lax.rem(i, 2)
         off = j + lax.div(j, 2) - 2 * lax.div(j, 3)
         return which * side + lax.rem(place.x * (1 - which) + place.y * which + off, side)
 
     def is_back(s):
-        return jnp.logical_or(jnp.logical_and(s >= 2, s < 4), s >= 10)
+        return s >= n_tile
 
     def swap_copy(s, kind, t):
         slot = lax.rem(s, 2)
@@ -296,10 +342,21 @@
         def _():
             take(1, part_dh)
 
+    def after(s, k, *actions):
+        @pl.when(s == k)
+        def _():
+            for action in actions:
+                action()
+
     def hand_over(s, kind, t, part, value):
         @pl.when(s >= 1)
         def _():
             settle(s - 1)
+
+        if kind == 1:
+            after(s, n_tile, scat_y.begin)
+            after(s, n_tile + 2, scat_dh.begin_far)
+            after(s, n_tile + 6, scat_dh.begin_near)
 
         @pl.when(s >= 2)
         def _():
@@ -309,28 +366,24 @@
         stage[slot] = value().astype(BF16)
         part[t] = stage[slot, mine]
         if kind == 1:
-            pl.semaphore_wait(credit, 1)
+            @pl.when(s == n_tile)
+            def _():
+                pl.semaphore_wait(credit, n_tile)
         swap_copy(s, kind, t).start()
 
     def tile_step(s, _):
         t = index_of(s)
 
-        def at(k, *actions):
-            @pl.when(s == k)
-            def _():
-                for action in actions:
-                    action()
-
-        at(0, lambda: gather_h.wait(10))
-        at(2, gather_h.relay_major, gather_dy.send_major, lambda: gather_dy.wait(10))
-        at(4, gather_h.share_near, lambda: gather_h.wait(11, 12, 13, 14))
-        at(6, gather_h.share_far)
-        at(7, gather_dy.relay_major)
-        at(8, lambda: gather_h.wait(15, 16))
-        at(10, gather_dy.share_near, lambda: gather_dy.wait(11, 12, 13, 14))
-        at(11, scat_y.begin)
-        at(12, gather_dy.share_far)
-        at(14, lambda: gather_dy.wait(15, 16), scat_y.relay_major)
+        after(s, 0, lambda: gather_h.wait(10))
+        after(s, 1, gather_dy.share_own)
+        after(s, 2, gather_h.relay_major, gather_dy.send_major, gather_h.share_near, lambda: gather_h.wait(11, 12, 13, 14))
+        after(s, 5, gather_h.share_far)
+        after(s, 6, gather_dy.relay_major, lambda: gather_h.wait(15, 16))
+        after(s, 7, gather_dy.share_near)
+        after(s, 8, gather_dy.share_far, lambda: gather_dy.wait(15, 16))
+        after(s, 10, lambda: gather_dy.wait(11, 12, 13, 14))
+        after(s, 11, scat_y.relay_major)
+        after(s, 14, scat_y.turn, lambda: gather_dy.wait(10))
 
         @pl.when(jnp.logical_not(is_back(s)))
         def _():
@@ -367,7 +420,8 @@
 
     gather_dg.begin(local.at[2])
     settle(steps - 1)
-    scat_dh.begin()
+    scat_dh.relay_major()
+    scat_y.relay_minor()
     d_bias[...] = jnp.sum(bias_s[...], axis=0)
 
     m_blk = tile_rows
@@ -387,24 +441,18 @@
         for cp in wide_copies(mb):
             cp.start()
 
-        def after(k, *actions):
-            @pl.when(mb == k)
-            def _():
-                for action in actions:
-                    action()
-
-        after(0, lambda: gather_dg.relay_minor(local.at[2]), scat_y.turn)
-        after(1, gather_dg.share_own, gather_dg.send_major)
-        after(2, scat_y.relay_minor, scat_dh.relay_major)
-        after(4, gather_dg.relay_major)
-        after(5, gather_dg.share_near)
+        after(mb, 0, lambda: gather_dg.relay_minor(local.at[2]))
+        after(mb, 1, gather_dg.share_own, gather_dg.send_major)
+        after(mb, 3, scat_dh.turn)
+        after(mb, 4, gather_dg.relay_major)
+        after(mb, 5, scat_dh.relay_minor, gather_dg.share_near)
         return 0
 
     lax.fori_loop(0, n_m, wide_step, 0)
 
     for h in halves:
         r = pl.ds(h.which * blk, blk)
-        y_ref[r] = (x_ref[r].astype(F32) + scat_y.total(h) + bias_ref[...].astype(F32)).astype(BF16)
+        y_ref[r] = (x_ref[r].astype(F32) + scat_y.total(h) + row_f32(bias_ref)).astype(BF16)
 
     n_blk = wd_s.shape[2]
     n_n = d // n_blk
@@ -424,17 +472,7 @@
         for cp in down_copies(nb):
             cp.start()
 
-        @pl.when(nb == 0)
-        def _():
-            gather_dg.share_far()
-
-        @pl.when(nb == 2)
-        def _():
-            scat_dh.turn()
-
-        @pl.when(nb == 4)
-        def _():
-            scat_dh.relay_minor()
+        after(nb, 0, gather_dg.share_far)
         return 0
 
     lax.fori_loop(0, n_n, down_step, 0)
@@ -459,9 +497,9 @@
         d_l = (g_t * (d_g - jnp.sum(g_t * d_g, axis=0, keepdims=True))).astype(BF16)
         dl_s[t] = d_l
         dr_s[...] += jnp.dot(d_l, hid[t, :, pl.ds(0, d)], preferred_element_type=F32)
-    d_router_t[...] = jnp.dot(pick[...], dr_s[...], preferred_element_type=F32, precision=lax.Precision.HIGHEST)
-
-    gain = gain_ref[...].astype(F32)
+    d_router_t[...] = jnp.dot(one_hot(pick, F32), dr_s[...], preferred_element_type=F32, precision=lax.Precision.HIGHEST)
+
+    gain = row_f32(gain_ref)
     gain_part = jnp.zeros((1, d), F32)
     for h in halves:
         r = pl.ds(h.which * blk, blk)
@@ -509,7 +547,7 @@
             cp.wait()
 
 
-def moe(mesh, h_ext, dy, x_in, gain, bias, sel, sel_t, w_rt, pick, w_gate, w_up, w_down):
+def moe(mesh, dy, x_in, gain, bias, w_r, idx, w_gate, w_up, w_down):
     side = mesh.shape["tp"]
     n_tok, d = dy.shape
     e_loc, _, ff = w_gate.shape
@@ -518,7 +556,7 @@
     n_tile = 2 * side
     n_ep = side * CORES
     n_exp = n_ep * e_loc
-    dx = h_ext.shape[1]
+    dx = d + 128
     vm = pl.BlockSpec(memory_space=pltpu.VMEM)
     hbm = pl.BlockSpec(memory_space=pl.ANY)
     blk = n_tok // 2
@@ -536,7 +574,7 @@
             jax.ShapeDtypeStruct(w_up.shape, F32),
             jax.ShapeDtypeStruct(w_down.shape, F32),
         ),
-        in_specs=[vm] * 9 + [hbm] * 3,
+        in_specs=[vm] * 6 + [hbm] * 3,
         out_specs=(vm, vm, vm, vm, vm, hbm, hbm, hbm),
         scratch_shapes=[
             pltpu.VMEM((n_tile, tile_rows, dx), BF16),
@@ -564,6 +602,10 @@
             pltpu.VMEM((n_ep * 8, d), F32),
             pltpu.VMEM((n_ep, 1, d), F32),
             pltpu.VMEM((side, 1, d), F32),
+            pltpu.VMEM((n_tok, dx), BF16),
+            pltpu.VMEM((128, e_loc * ff), BF16),
+            pltpu.VMEM((n_ep * 8, 128), BF16),
+            pltpu.VMEM((n_ep * 8, d), BF16),
             pltpu.SemaphoreType.DMA((3 * e_loc,)),
             pltpu.SemaphoreType.DMA((3, 2)),
             pltpu.SemaphoreType.DMA((3, n_g)),
@@ -579,7 +621,7 @@
         ],
         compiler_params=pltpu.CompilerParams(collective_id=0, has_side_effects=True, vmem_limit_bytes=67043328),
         name="moe",
-    )(h_ext, dy, x_in, gain, bias, sel, sel_t, w_rt, pick, w_gate, w_up, w_down)
+    )(dy, x_in, gain, bias, w_r, idx, w_gate, w_up, w_down)
 
 
 def solution(mesh):
@@ -592,35 +634,8 @@
     assert mesh.shape["ep"] == side * CORES
 
     def device_step(x_in, norm_gain, w_router, expert_idx, w_gate, w_up, w_down, out_bias, dy_out):
-        n_tok, d_model = x_in.shape
-        n_exp = w_router.shape[1]
-        local_exp, _, ff = w_gate.shape
-        n_ep = n_exp // local_exp
-        x_f32 = x_in.astype(F32)
-        inv_rms = lax.rsqrt(jnp.mean(x_f32 * x_f32, axis=-1, keepdims=True) + EPS)
-        hidden = (x_f32 * inv_rms * norm_gain.astype(F32)).astype(BF16)
-        logits = jnp.dot(hidden, w_router, preferred_element_type=F32)
-        chosen = expert_idx[:, :, None] == jnp.arange(n_exp)[None, None, :]
-        mask = jnp.any(chosen, axis=1)
-        top = jnp.max(jnp.where(mask, logits, -jnp.inf), axis=-1, keepdims=True)
-        unnorm = jnp.where(mask, jnp.exp(jnp.minimum(logits - top, 0.0)), 0.0)
-        gates = unnorm / jnp.sum(unnorm, axis=-1, keepdims=True)
-        hi = lax.reduce_precision(gates, 8, 7)
-        mid = lax.reduce_precision(gates - hi, 8, 7)
-        lo = gates - hi - mid
-        zeros = jnp.zeros((n_tok, 128 - 3 * n_exp), F32)
-        h_ext = jnp.concatenate([hidden, jnp.concatenate([hi, mid, lo, zeros], axis=1).astype(BF16)], axis=1)
-        ep = lax.axis_index("ep")
-        lane = jnp.arange(128)
-        lane_e = jnp.where(lane < 3 * n_exp, lane % n_exp, n_exp)
-        sel = (lane_e[:, None] == (ep * local_exp + jnp.arange(local_exp * ff) // ff)[None, :]).astype(BF16)
-        slot = jnp.arange(n_ep * 8)
-        slot_e = jnp.where(slot % 8 < local_exp, slot // 8 * local_exp + slot % 8, n_exp + 1)
-        sel_t = (slot_e[:, None] == lane_e[None, :]).astype(BF16)
-        pick = (jnp.arange(n_exp)[:, None] == slot_e[None, :]).astype(F32)
-        w_rt = jnp.pad(w_router.T.reshape(n_ep, local_exp, d_model), ((0, 0), (0, 8 - local_exp), (0, 0))).reshape(n_ep * 8, d_model)
-        row = lambda v: v.reshape(1, d_model)
-        y_out, dx_in, d_gain, d_bias, d_router_t, d_gate, d_up, d_down = moe(mesh, h_ext, dy_out, x_in, row(norm_gain), row(out_bias), sel, sel_t, w_rt, pick, w_gate, w_up, w_down)
+        d_model = x_in.shape[1]
+        y_out, dx_in, d_gain, d_bias, d_router_t, d_gate, d_up, d_down = moe(mesh, dy_out, x_in, norm_gain, out_bias, w_router.T, expert_idx, w_gate, w_up, w_down)
         return y_out, dx_in, d_gain.reshape(d_model), d_router_t.T, d_gate, d_up, d_down, d_bias.reshape(d_model)
 
     return jax.shard_map(device_step, mesh=mesh, in_specs=(tok_spec, P(None), P(None, None), tok_spec, wide_spec, wide_spec, down_spec, P(None), tok_spec), out_specs=(tok_spec, tok_spec, P("dp"), P("dp", None), grad_wide, grad_wide, grad_down, P("dp")), check_vma=False)

time: 151 us -> 137 us (0.907)
  other arithmetic: 8.53 us -> 2.62 us
  local copies, waits for them, and re-layouts: 20 us -> 16.2 us
  Pallas kernels: 120 us -> 117 us
    reshape x4 -> x0, local copies, waits for them, and re-layouts: 4.24 us -> none  [the longest x2 2.57 us: device_step(): row = lambda v: v.reshape(1, d_model)]
    convert_element_type x5 -> x0, other arithmetic: 3.8 us -> none  [the longest x2 1.74 us: device_step(): hidden = (x_f32 * inv_rms * norm_gain.astype(F32)).astype(BF16)]
    pallas_call x1, Pallas kernels: 120 us -> 117 us  [moe(): pl.pallas_call(functools.partial(moe_kernel, side, d, e_loc, ff, n_exp),...]
    unnamed x10 -> x11, local copies, waits for them, and re-layouts: 14.8 us -> 16.2 us
where the time goes in v4:
time: 137 us
  Pallas kernels  117 us (85%)
  local copies, waits for them, and re-layouts  16.2 us (12%)
  other arithmetic  2.62 us (2%)
    pallas_call x1, Pallas kernels, moe(): pl.pallas_call(functools.partial(moe_kernel, side, d, e_loc, ff, n_exp),...  117 us
    unnamed x11, local copies, waits for them, and re-layouts  16.2 us

profile of v4, /device:TPU:97, one launch (start us, length us, event | category | flops | bytes accessed | tf_op | source)
XLA Modules:
  0.0 136.8 jit_solution(13559359835032601936)
XLA Ops:
  0.6 1.4 %copy.17.idx_ref = s32[64,8]{1,0:T(8,128)} copy(s32[64,8]{0,1:T(8,128)} %param.12) | data formatting | bytes 4096 | tf_op args[3]
  2.0 117.3 %moe.1 = (bf16[64,1536]{1,0:T(8,128)(2,1)}, bf16[64,1536]{1,0:T(8,128)(2,1)}, f32[1,1536]{1,0:T(1,128)}, f32[1,1536]{1,0:T(1,128)}, f32[40,1536]{1,0:T(8,128)}, ...) custom-call(bf16[64,1536]{1,0:T(8,128)(2,1)} %dy_in.1, bf16[64,1536]{1,0:T(8,128)(2,1)} %x_ref.1, ...), custom_call_target="tpu_custom_call" | custom-call | tf_op jit(solution)/shard_map/moe/pallas_call | solution.py:565
  119.4 1.3 reduce
  120.7 1.3 reduce.1
  122.0 1.6 %copy.24 = bf16[64,1536]{1,0:T(8,128)(2,1)} copy(bf16[64,1536]{1,0:T(8,128)(2,1)} %get-tuple-element.32) | data formatting | bytes 393216
  123.6 1.6 %copy.25 = bf16[64,1536]{1,0:T(8,128)(2,1)} copy(bf16[64,1536]{1,0:T(8,128)(2,1)} %get-tuple-element.33) | data formatting | bytes 393216
  125.2 1.7 %copy.26 = f32[1536,40]{0,1:T(8,128)} copy(f32[1536,40]{0,1:T(8,128)} %bitcast.2) | data formatting | bytes 491520
  126.9 0.0 copy-start.1
  126.9 4.4 %copy.27 = f32[5,1536,128]{2,1,0:T(8,128)} copy(f32[5,1536,128]{2,1,0:T(8,128)} %get-tuple-element.36) | data formatting | bytes 7864320
  131.3 0.0 copy-done.1
  131.3 0.0 copy-start
  131.3 2.0 %copy.28 = f32[5,1536,128]{2,1,0:T(8,128)} copy(f32[5,1536,128]{2,1,0:T(8,128)S(1)} %copy-done.1) | data formatting | bytes 7864320
  133.3 1.5 %copy-done = f32[5,128,1536]{2,1,0:T(8,128)S(1)} copy-done((f32[5,128,1536]{2,1,0:T(8,128)S(1)}, f32[5,128,1536]{2,1,0:T(8,128)}, u32[]{:S(2)}) %copy-start) | copy-done | bytes 3932184
  134.8 1.9 %copy.29 = f32[5,128,1536]{2,1,0:T(8,128)} copy(f32[5,128,1536]{2,1,0:T(8,128)S(1)} %copy-done) | data formatting | bytes 7864320
Async XLA Ops:
  126.9 4.4 %copy-start.1 = (f32[5,1536,128]{2,1,0:T(8,128)S(1)}, f32[5,1536,128]{2,1,0:T(8,128)}, u32[]{:S(2)}) copy-start(f32[5,1536,128]{2,1,0:T(8,128)} %get-tuple-element.37) | copy-start | bytes 11796484
  131.3 3.5 %copy-start = (f32[5,128,1536]{2,1,0:T(8,128)S(1)}, f32[5,128,1536]{2,1,0:T(8,128)}, u32[]{:S(2)}) copy-start(f32[5,128,1536]{2,1,0:T(8,128)} %get-tuple-element.38) | copy-start | bytes 11796484

commit v5 on v4

--- a/solution.py
+++ b/solution.py
@@ -55,7 +55,8 @@
 
 
 class Gather:
-    COPIES = 17
+    COPIES = 20
+    OFFSETS = (0, -1, 1, 2)
 
     def __init__(self, halves, own, buf, send, recv):
         self.halves, self.own, self.buf, self.send, self.recv = halves, own, buf, send, recv
@@ -68,20 +69,15 @@
         b, p = self.buf, h.p
         same = lambda t, r, target: self.copy(h, k, b.at[t, r], b.at[t, r], target)
         s, d = 1 - 2 * (k % 2), k % 2
-        if k < 2:
-            return self.copy(h, k, self.own.at[pl.ds(h.which * h.blk, h.blk)], b.at[h.tile(0), h.block(0)], p.along(h.minor, s))
-        if k < 4:
+        if k in (2, 3):
             return same(h.tile(0), h.block(-s, d, 2), p.along(h.minor, s))
         if k < 6:
-            return same(h.tile(0), h.mine(d, 2), p.along(h.major, s))
-        if k < 8:
-            return same(h.tile(0), h.mine(1 - d, 2), p.along(h.major, s))
-        if k < 10:
-            return same(h.tile(-s), h.mine(d, 2), p.along(h.major, s))
-        if k == 10:
-            return same(h.tile(0), h.mine(), p.partner())
-        step, part = ((-1, 0), (1, 1), (-1, 1), (1, 0), (2, 0), (2, 1))[k - 11]
-        return same(h.tile(step), h.mine(part, 2), p.partner())
+            return self.copy(h, k, self.own.at[pl.ds(h.which * h.blk, h.blk)], b.at[h.tile(0), h.block(0)], p.along(h.minor if k < 2 else h.major, s))
+        if k < 12:
+            return same(h.tile(0), h.block(self.OFFSETS[(k - 4) // 2]), p.along(h.major, s))
+        if k < 16:
+            return same(h.tile(-s), h.block((0, 1, -1, 2)[k - 12]), p.along(h.major, s))
+        return same(h.tile((0, -1, 1, 2)[k - 16]), h.mine(), p.partner())
 
     def own_copy(self, h, sem):
         return pltpu.make_async_copy(self.own.at[pl.ds(h.which * h.blk, h.blk)], self.buf.at[h.tile(0), h.block(0)], sem)
@@ -102,7 +98,7 @@
                 self.make(h, k).wait_send()
 
     def begin(self, local):
-        self.start(0, 1)
+        self.start(0, 1, 4, 5)
         for h in self.halves:
             self.own_copy(h, local.at[h.which]).start()
 
@@ -110,26 +106,29 @@
         for h in self.halves:
             self.own_copy(h, local.at[h.which]).wait()
         self.wait(0, 1)
-        self.start(2, 3)
+        self.start(2, 3, 6, 7, 8, 9)
+        self.wait(4)
+        self.start(12)
 
     def share_own(self):
         self.wait(2, 3)
-        self.start(10)
-
-    def send_major(self):
-        self.start(4, 5, 6, 7)
+        self.start(10, 11, 16)
 
     def relay_major(self):
-        self.wait(4, 5)
-        self.start(8, 9, 11, 12)
+        self.wait(6)
+        self.start(14)
+        self.wait(9)
+        self.start(13)
 
     def share_near(self):
-        self.wait(6, 7)
-        self.start(13, 14)
+        self.wait(11)
+        self.start(15)
+        self.wait(8, 10, 5, 7)
+        self.start(17, 18)
 
     def share_far(self):
-        self.wait(8, 9)
-        self.start(15, 16)
+        self.wait(12, 13, 14, 15)
+        self.start(19)
 
 
 class Scatter:
@@ -304,9 +303,7 @@
     pick = slot_expert((n_exp, 8 * n_ep), 1) == expert_row((n_exp, 8 * n_ep))
     w_rt[...] = lax.dot_general(one_hot(pick), w_r[...], TN, preferred_element_type=F32).astype(BF16)
     gather_h.relay_minor(local.at[0])
-    gather_dy.relay_minor(local.at[1])
     gather_h.share_own()
-    gather_h.send_major()
     for w in weights:
         w.wait()
 
@@ -314,7 +311,10 @@
 
     def index_of(s):
         back = lax.div(s, n_tile)
-        i = s * (1 - back) + (2 * n_tile - 1 - s) * back
+        r = s - n_tile
+        late = lax.div(r, 2)
+        j_back = jnp.where(late == 0, 1, jnp.where(late == 1, 3, jnp.where(late == 2, 2, 0)))
+        i = jnp.where(back == 0, s, 2 * j_back + lax.rem(r, 2))
         j, which = lax.div(i, 2), lax.rem(i, 2)
         off = j + lax.div(j, 2) - 2 * lax.div(j, 3)
         return which * side + lax.rem(place.x * (1 - which) + place.y * which + off, side)
@@ -355,7 +355,7 @@
 
         if kind == 1:
             after(s, n_tile, scat_y.begin)
-            after(s, n_tile + 2, scat_dh.begin_far)
+            after(s, n_tile + 4, scat_dh.begin_far)
             after(s, n_tile + 6, scat_dh.begin_near)
 
         @pl.when(s >= 2)
@@ -374,16 +374,18 @@
     def tile_step(s, _):
         t = index_of(s)
 
-        after(s, 0, lambda: gather_h.wait(10))
-        after(s, 1, gather_dy.share_own)
-        after(s, 2, gather_h.relay_major, gather_dy.send_major, gather_h.share_near, lambda: gather_h.wait(11, 12, 13, 14))
-        after(s, 5, gather_h.share_far)
-        after(s, 6, gather_dy.relay_major, lambda: gather_h.wait(15, 16))
-        after(s, 7, gather_dy.share_near)
-        after(s, 8, gather_dy.share_far, lambda: gather_dy.wait(15, 16))
-        after(s, 10, lambda: gather_dy.wait(11, 12, 13, 14))
+        after(s, 0, lambda: gather_h.wait(16))
+        after(s, 1, gather_h.relay_major, lambda: gather_dy.relay_minor(local.at[1]))
+        after(s, 2, gather_h.share_near, lambda: gather_h.wait(17, 18))
+        after(s, 3, gather_dy.share_own)
+        after(s, 4, gather_h.share_far, gather_dy.relay_major)
+        after(s, 6, lambda: gather_h.wait(19), gather_dy.share_near)
+        after(s, 8, gather_dy.share_far, lambda: gather_dy.wait(17, 18))
+        after(s, 10, lambda: gather_dy.wait(19))
         after(s, 11, scat_y.relay_major)
-        after(s, 14, scat_y.turn, lambda: gather_dy.wait(10))
+        after(s, 13, scat_y.turn)
+        after(s, 14, lambda: gather_dy.wait(16))
+        after(s, 15, scat_dh.relay_major, scat_y.relay_minor)
 
         @pl.when(jnp.logical_not(is_back(s)))
         def _():
@@ -420,8 +422,6 @@
 
     gather_dg.begin(local.at[2])
     settle(steps - 1)
-    scat_dh.relay_major()
-    scat_y.relay_minor()
     d_bias[...] = jnp.sum(bias_s[...], axis=0)
 
     m_blk = tile_rows
@@ -442,17 +442,13 @@
             cp.start()
 
         after(mb, 0, lambda: gather_dg.relay_minor(local.at[2]))
-        after(mb, 1, gather_dg.share_own, gather_dg.send_major)
+        after(mb, 2, gather_dg.share_own)
         after(mb, 3, scat_dh.turn)
         after(mb, 4, gather_dg.relay_major)
-        after(mb, 5, scat_dh.relay_minor, gather_dg.share_near)
+        after(mb, 5, gather_dg.share_near)
         return 0
 
     lax.fori_loop(0, n_m, wide_step, 0)
-
-    for h in halves:
-        r = pl.ds(h.which * blk, blk)
-        y_ref[r] = (x_ref[r].astype(F32) + scat_y.total(h) + row_f32(bias_ref)).astype(BF16)
 
     n_blk = wd_s.shape[2]
     n_n = d // n_blk
@@ -472,13 +468,18 @@
         for cp in down_copies(nb):
             cp.start()
 
-        after(nb, 0, gather_dg.share_far)
         return 0
 
-    lax.fori_loop(0, n_n, down_step, 0)
-
-    gather_dg.wait(10, 11, 12, 13, 14, 15, 16)
-    dr_s[...] = jnp.zeros_like(dr_s)
+    early = n_n // 3
+    lax.fori_loop(0, early, down_step, 0)
+    scat_dh.relay_minor()
+    gather_dg.share_far()
+
+    for h in halves:
+        r = pl.ds(h.which * blk, blk)
+        y_ref[r] = (x_ref[r].astype(F32) + scat_y.total(h) + row_f32(bias_ref)).astype(BF16)
+
+    gather_dg.wait(16, 17, 18, 19)
     for t in range(n_tile):
         which, tl = t // side, t % side
         pieces = []
@@ -496,8 +497,6 @@
         g_t = lax.dot_general(sel_t[...], hid[t, :, pl.ds(d, 128)], NT, preferred_element_type=F32)
         d_l = (g_t * (d_g - jnp.sum(g_t * d_g, axis=0, keepdims=True))).astype(BF16)
         dl_s[t] = d_l
-        dr_s[...] += jnp.dot(d_l, hid[t, :, pl.ds(0, d)], preferred_element_type=F32)
-    d_router_t[...] = jnp.dot(one_hot(pick, F32), dr_s[...], preferred_element_type=F32, precision=lax.Precision.HIGHEST)
 
     gain = row_f32(gain_ref)
     gain_part = jnp.zeros((1, d), F32)
@@ -516,22 +515,28 @@
         dx_ref[r] = (dy_in[r].astype(F32) + inv_rms * (d_norm - normed * jnp.mean(d_norm * normed, axis=1, keepdims=True))).astype(BF16)
 
     def spread(buf, slot, peers, first):
-        out = []
-        for o, peer in enumerate(peers):
-            out.append(pltpu.make_async_remote_copy(src_ref=buf.at[slot], dst_ref=buf.at[slot], send_sem=ar_send.at[first + o], recv_sem=ar_recv.at[first + o], device_id=peer, device_id_type=MESH))
-        for cp in out:
-            cp.start()
-        for cp in out:
-            cp.wait_recv()
-        return out
+        return [pltpu.make_async_remote_copy(src_ref=buf.at[slot], dst_ref=buf.at[slot], send_sem=ar_send.at[first + o], recv_sem=ar_recv.at[first + o], device_id=peer, device_id_type=MESH) for o, peer in enumerate(peers)]
 
     ar1[me_ep] = gain_part
-    sent = spread(ar1, me_ep, ep_peers, 0)
+    over_ep = spread(ar1, me_ep, ep_peers, 0)
+    for cp in over_ep:
+        cp.start()
+    dr_s[...] = jnp.zeros_like(dr_s)
+    for t in range(n_tile):
+        dr_s[...] += jnp.dot(dl_s[t], hid[t, :, pl.ds(0, d)], preferred_element_type=F32)
+    for cp in over_ep:
+        cp.wait_recv()
     ar2[place.y] = jnp.sum(ar1[...], axis=0)
-    sent += spread(ar2, place.y, tp_peers, n_ep - 1)
+    over_tp = spread(ar2, place.y, tp_peers, n_ep - 1)
+    for cp in over_tp:
+        cp.start()
+    d_router_t[...] = jnp.dot(one_hot(pick, F32), dr_s[...], preferred_element_type=F32, precision=lax.Precision.HIGHEST)
+    lax.fori_loop(early, n_n, down_step, 0)
+    for cp in over_tp:
+        cp.wait_recv()
     d_gain[...] = jnp.sum(ar2[...], axis=0)
 
-    for cp in sent:
+    for cp in over_ep + over_tp:
         cp.wait_send()
     for g in (gather_h, gather_dy, gather_dg):
         g.finish()
@@ -624,6 +629,34 @@
     )(dy, x_in, gain, bias, w_r, idx, w_gate, w_up, w_down)
 
 
+def emit_kernel(*refs):
+    n = len(refs) // 2
+    for src, dst in zip(refs[:3], refs[n:n + 3]):
+        dst[...] = src[...]
+
+    @pl.when(pl.program_id(0) == 0)
+    def _():
+        for src, dst in zip(refs[3:n], refs[n + 3:]):
+            dst[...] = src[...].reshape(dst.shape)
+
+
+def emit(wide_a, wide_b, down, *small):
+    e_loc, d, ff = wide_a.shape
+    n = d // 256
+    wide = pl.BlockSpec((e_loc, 256, ff), lambda i: (0, i, 0))
+    deep = pl.BlockSpec((e_loc, ff, 256), lambda i: (0, 0, i))
+    whole = lambda v: pl.BlockSpec(v.shape, lambda i: (0,) * len(v.shape))
+    shapes = [jax.ShapeDtypeStruct(v.shape if v.shape[0] > 1 else (v.shape[1],), v.dtype) for v in small]
+    return pl.pallas_call(
+        emit_kernel,
+        grid=(n,),
+        out_shape=tuple(jax.ShapeDtypeStruct(v.shape, v.dtype) for v in (wide_a, wide_b, down)) + tuple(shapes),
+        in_specs=[wide, wide, deep] + [whole(v) for v in small],
+        out_specs=(wide, wide, deep) + tuple(whole(v) for v in shapes),
+        name="emit",
+    )(wide_a, wide_b, down, *small)
+
+
 def solution(mesh):
     tok_spec = P(("dp", "ep", "tp"), None)
     wide_spec = P("ep", None, "tp")
@@ -634,8 +667,8 @@
     assert mesh.shape["ep"] == side * CORES
 
     def device_step(x_in, norm_gain, w_router, expert_idx, w_gate, w_up, w_down, out_bias, dy_out):
-        d_model = x_in.shape[1]
         y_out, dx_in, d_gain, d_bias, d_router_t, d_gate, d_up, d_down = moe(mesh, dy_out, x_in, norm_gain, out_bias, w_router.T, expert_idx, w_gate, w_up, w_down)
-        return y_out, dx_in, d_gain.reshape(d_model), d_router_t.T, d_gate, d_up, d_down, d_bias.reshape(d_model)
+        d_gate, d_up, d_down, y_out, dx_in, d_gain, d_bias, d_router_t = emit(d_gate, d_up, d_down, y_out, dx_in, d_gain, d_bias, d_router_t)
+        return y_out, dx_in, d_gain, d_router_t.T, d_gate, d_up, d_down, d_bias
 
     return jax.shard_map(device_step, mesh=mesh, in_specs=(tok_spec, P(None), P(None, None), tok_spec, wide_spec, wide_spec, down_spec, P(None), tok_spec), out_specs=(tok_spec, tok_spec, P("dp"), P("dp", None), grad_wide, grad_wide, grad_down, P("dp")), check_vma=False)

time: 137 us -> 127 us (0.927)
  local copies, waits for them, and re-layouts: 16.2 us -> 1.38 us
  Pallas kernels: 117 us -> 125 us
  other arithmetic: 2.62 us -> 0 us
    unnamed x11 -> x1, local copies, waits for them, and re-layouts: 16.2 us -> 1.38 us
    pallas_call x0 -> x1, Pallas kernels: none -> 10.3 us  [emit(): pl.pallas_call(emit_kernel, grid=(n,), out_shape=tuple((jax.ShapeDtypeStr...]
    pallas_call x1, Pallas kernels: 117 us -> 114 us  [moe(): pl.pallas_call(functools.partial(moe_kernel, side, d, e_loc, ff, n_exp),...]
    pallas_call x2 -> x0, other arithmetic: 2.62 us -> none  [moe(): pl.pallas_call(functools.partial(moe_kernel, side, d, e_loc, ff, n_exp),...]
where the time goes in v5:
time: 127 us
  Pallas kernels  125 us (98%)
  local copies, waits for them, and re-layouts  1.38 us (1%)
    pallas_call x1, Pallas kernels, moe(): pl.pallas_call(functools.partial(moe_kernel, side, d, e_loc, ff, n_exp),...  114 us
    pallas_call x1, Pallas kernels, emit(): pl.pallas_call(emit_kernel, grid=(n,), out_shape=tuple((jax.ShapeDtypeStr...  10.3 us

profile of v5, /device:TPU:97, one launch (start us, length us, event | category | flops | bytes accessed | tf_op | source)
XLA Modules:
  0.0 127.0 jit_solution(13821253586970260305)
XLA Ops:
  0.6 1.4 %copy.17.idx_ref = s32[64,8]{1,0:T(8,128)} copy(s32[64,8]{0,1:T(8,128)} %param.12) | data formatting | bytes 4096 | tf_op args[3]
  2.0 114.5 %moe.1 = (bf16[64,1536]{1,0:T(8,128)(2,1)}, bf16[64,1536]{1,0:T(8,128)(2,1)}, f32[1,1536]{1,0:T(1,128)}, f32[1,1536]{1,0:T(1,128)}, f32[40,1536]{1,0:T(8,128)}, ...) custom-call(bf16[64,1536]{1,0:T(8,128)(2,1)} %dy_in.1, bf16[64,1536]{1,0:T(8,128)(2,1)} %x_ref.1, ...), custom_call_target="tpu_custom_call" | custom-call | tf_op jit(solution)/shard_map/moe/pallas_call | solution.py:570
  116.5 10.3 %emit.1 = (f32[5,1536,128]{2,1,0:T(8,128)}, f32[5,1536,128]{2,1,0:T(8,128)}, f32[5,128,1536]{2,1,0:T(8,128)}, bf16[64,1536]{1,0:T(8,128)(2,1)}, bf16[64,1536]{1,...) custom-call(f32[5,1536,128]{2,1,0:T(8,128)} %get-tuple-element.24.refs_0_, ...), custom_call_target="tpu_custom_call" | custom-call | tf_op jit(solution)/shard_map/emit/pallas_call | solution.py:650
